TPU v7x, 16 devices: a 4x2x1 block of a 4x4x8 slice. The times are simulated.
16 devices in a mesh: dp: 2 (over y, z), ep: 8 (over x, core).
Axes of the slice: x: 4, y: 2, z: 1, core: 2. Of those that a mesh axis runs over, the one named last changes fastest.
The devices are a block of a 4x4x8 slice.
Arguments:
- hidden: bfloat16 [16, 128, 1024], P(('dp', 'ep')), parts along dimension 0
- expert_ids: int32 [16, 128, 8], P(('dp', 'ep')), parts along dimension 0
- slot_ids: int32 [16, 128, 8], P(('dp', 'ep')), parts along dimension 0
- attn_norm: bfloat16 [1024], replicated
- w_query: bfloat16 [1024, 1024], replicated
- w_key: bfloat16 [1024, 512], replicated
- w_value: bfloat16 [1024, 512], replicated
- w_out: bfloat16 [16, 64, 1024], replicated
- ffn_norm: bfloat16 [1024], replicated
- ffn_gate: bfloat16 [1024, 4096], replicated
- ffn_up: bfloat16 [1024, 4096], replicated
- ffn_down: bfloat16 [4096, 1024], replicated
- moe_norm: bfloat16 [1024], replicated
- w_router: bfloat16 [1024, 32], replicated
- exp_gate: bfloat16 [32, 1024, 512], P('ep')
- exp_up: bfloat16 [32, 1024, 512], P('ep')
- exp_down: bfloat16 [32, 512, 1024], P('ep')
Outputs:
- output: bfloat16 [16, 128, 1024], P(('dp', 'ep')), parts along dimension 0
There are 2 independent parts. A program takes and returns all parts, laid end to end along the dimension named above; an argument that names none is the same for every part.
All inputs are finite; a program needn't handle non-finite values.
Results may differ from a plain program's by a relative error of at most 0.00945966.
Values are sent between devices in bfloat16 or wider.
A program may use at most 768 MiB of HBM per device.

v0:
```python
import jax
import jax.numpy as jnp
from jax import lax
from jax.sharding import PartitionSpec as P, NamedSharding

RMS_EPS = 1e-6
ROPE_BASE = 10000.0
CAP_FACTOR = 3


def rms_norm(row_vals, norm_scale):
    as_float = row_vals.astype(jnp.float32)
    inv_rms = lax.rsqrt(jnp.mean(as_float * as_float, axis=-1, keepdims=True) + RMS_EPS)
    return (as_float * inv_rms * norm_scale.astype(jnp.float32)).astype(jnp.bfloat16)


def rotary(head_vals):
    seq_len, head_dim = head_vals.shape[1], head_vals.shape[3]
    half_dim = head_dim // 2
    inv_freq = ROPE_BASE ** (-2.0 * jnp.arange(half_dim, dtype=jnp.float32) / head_dim)
    angles = jnp.arange(seq_len, dtype=jnp.float32)[:, None] * inv_freq[None, :]
    cos_t = jnp.cos(angles)[:, None, :]
    sin_t = jnp.sin(angles)[:, None, :]
    first_half = head_vals[..., :half_dim]
    second_half = head_vals[..., half_dim:]
    return jnp.concatenate([first_half * cos_t - second_half * sin_t, second_half * cos_t + first_half * sin_t], axis=-1)


def dense_branch(hidden, attn_norm, w_query, w_key, w_value, w_out, ffn_norm, ffn_gate, ffn_up, ffn_down):
    n_seqs, seq_len, model_dim = hidden.shape
    n_heads, head_dim = w_out.shape[0], w_out.shape[1]
    kv_heads = w_key.shape[1] // head_dim
    q_per_kv = n_heads // kv_heads
    normed = rms_norm(hidden, attn_norm)
    queries = rotary(jnp.einsum('bsd,de->bse', normed, w_query, preferred_element_type=jnp.float32).reshape(n_seqs, seq_len, n_heads, head_dim))
    queries = queries.astype(jnp.bfloat16).reshape(n_seqs, seq_len, kv_heads, q_per_kv, head_dim)
    key_vals = rotary(jnp.einsum('bsd,de->bse', normed, w_key, preferred_element_type=jnp.float32).reshape(n_seqs, seq_len, kv_heads, head_dim)).astype(jnp.bfloat16)
    values = jnp.einsum('bsd,de->bse', normed, w_value, preferred_element_type=jnp.float32).astype(jnp.bfloat16).reshape(n_seqs, seq_len, kv_heads, head_dim)
    scores = jnp.einsum('bsgrd,btgd->bgrst', queries, key_vals, preferred_element_type=jnp.float32) * head_dim ** -0.5
    causal = jnp.arange(seq_len)[:, None] >= jnp.arange(seq_len)[None, :]
    attn_prob = jax.nn.softmax(jnp.where(causal, scores, -jnp.inf), axis=-1).astype(jnp.bfloat16)
    context = jnp.einsum('bgrst,btgd->bsgrd', attn_prob, values, preferred_element_type=jnp.float32).astype(jnp.bfloat16)
    context = context.reshape(n_seqs, seq_len, n_heads, head_dim)
    attn_out = (hidden.astype(jnp.float32) + jnp.einsum('bshd,hde->bse', context, w_out, preferred_element_type=jnp.float32)).astype(jnp.bfloat16)
    normed_ffn = rms_norm(attn_out, ffn_norm)
    hidden_act = (jax.nn.silu(jnp.einsum('bsd,df->bsf', normed_ffn, ffn_gate, preferred_element_type=jnp.float32)) * jnp.einsum('bsd,df->bsf', normed_ffn, ffn_up, preferred_element_type=jnp.float32)).astype(jnp.bfloat16)
    return attn_out.astype(jnp.float32) + jnp.einsum('bsf,fd->bsd', hidden_act, ffn_down, preferred_element_type=jnp.float32)


def route_gates(normed, w_router, choice_ids):
    logits = jnp.einsum('...d,de->...e', normed, w_router, preferred_element_type=jnp.float32)
    return jax.nn.softmax(jnp.take_along_axis(logits, choice_ids, axis=-1), axis=-1)


def expert_ffn(expert_in, exp_gate, exp_up, exp_down):
    z_gate = jnp.einsum('egcd,edf->egcf', expert_in, exp_gate, preferred_element_type=jnp.float32)
    z_up = jnp.einsum('egcd,edf->egcf', expert_in, exp_up, preferred_element_type=jnp.float32)
    hidden_act = (jax.nn.silu(z_gate) * z_up).astype(jnp.bfloat16)
    return jnp.einsum('egcf,efd->egcd', hidden_act, exp_down, preferred_element_type=jnp.float32).astype(jnp.bfloat16)


def solution(mesh):
    group_size = mesh.shape['ep']
    row_spec = P(('dp', 'ep'), None, None)
    vec_spec = P(None)
    mat_spec = P(None, None)
    cube_spec = P(None, None, None)
    expert_spec = P('ep', None, None)

    def per_device(hidden, expert_ids, slot_ids, attn_norm, w_query, w_key, w_value, w_out, ffn_norm, ffn_gate, ffn_up, ffn_down, moe_norm, w_router, exp_gate, exp_up, exp_down):
        n_seqs, seq_len, model_dim = hidden.shape
        top_k = expert_ids.shape[-1]
        tokens = n_seqs * seq_len
        local_experts = exp_gate.shape[0]
        n_experts = local_experts * group_size
        capacity = CAP_FACTOR * tokens * top_k // n_experts
        normed = rms_norm(hidden.reshape(tokens, model_dim), moe_norm)
        choice_ids = expert_ids.reshape(tokens, top_k)
        gate_vals = route_gates(normed, w_router, choice_ids)
        buf_pos = choice_ids * capacity + slot_ids.reshape(tokens, top_k)
        owner_tok = jnp.full((n_experts * capacity,), tokens, jnp.int32).at[buf_pos.reshape(-1)].set(jnp.arange(tokens * top_k, dtype=jnp.int32) // top_k)
        padded = jnp.concatenate([normed, jnp.zeros((1, model_dim), jnp.bfloat16)], axis=0)
        send_buf = jnp.take(padded, owner_tok, axis=0).reshape(group_size, local_experts, capacity, model_dim)
        recv_buf = lax.all_to_all(send_buf, 'ep', 0, 1)
        expert_out = expert_ffn(recv_buf, exp_gate, exp_up, exp_down)
        back_buf = lax.all_to_all(expert_out, 'ep', 1, 0).reshape(n_experts * capacity, model_dim)
        picked = jnp.take(back_buf, buf_pos.reshape(-1), axis=0).reshape(tokens, top_k, model_dim)
        moe_out = jnp.sum(gate_vals[:, :, None] * picked.astype(jnp.float32), axis=1)
        dense_out = dense_branch(hidden, attn_norm, w_query, w_key, w_value, w_out, ffn_norm, ffn_gate, ffn_up, ffn_down).reshape(tokens, model_dim)
        return (dense_out + moe_out).astype(jnp.bfloat16).reshape(n_seqs, seq_len, model_dim)

    return jax.shard_map(per_device, mesh=mesh, in_specs=(row_spec, row_spec, row_spec, vec_spec, mat_spec, mat_spec, mat_spec, cube_spec, vec_spec, mat_spec, mat_spec, mat_spec, vec_spec, mat_spec, expert_spec, expert_spec, expert_spec), out_specs=row_spec, check_vma=False)
```

profile of v0, /device:TPU:112, one launch (start us, length us, event | category | flops | bytes accessed | tf_op | source)
XLA Modules:
  0.0 231.1 jit_solution(11654876563399880492)
XLA Ops:
  0.0 0.0 copy-start
  0.0 0.9 multiply_add_fusion
  0.9 0.1 copy.42
  1.0 0.1 add.144
  1.1 4.3 %scatter_custom_fusion = s32[3072]{0:T(1024)S(1)} fusion(s32[1024]{0:T(1024)S(1)} %bitcast.181, s32[1024]{0:T(1024)S(1)} %add_select_fusion, s32[]{:T(128)} %constant.90.clone.1), kind=kCustom, calls=%fused_computation.98 | custom fusion | bytes 12292 | tf_op jit(solution)/shard_map/scatter | solution.py:81
  5.4 1.1 fusion.34
  6.5 0.7 convert_element_type.92
  7.2 0.1 broadcast_in_dim.66
  7.3 1.1 fusion.36
  8.4 14.0 %gather_fusion = bf16[3072,1024]{1,0:T(8,128)(2,1)} fusion(bf16[129,1024]{1,0:T(8,128)(2,1)S(1)} %concatenate.32, s32[3072]{0:T(1024)S(1)} %fusion.66), kind=kCustom, calls=%fused_computation | custom fusion | bytes 12595200 | tf_op jit(solution)/shard_map/jit(_take)/gather | solution.py:83
  22.4 3.8 %select_bitcast_fusion = bf16[8,4,1,96,1024]{4,3,1,2,0:T(8,128)(2,1)S(1)} fusion(bf16[8,4,1,96,1024]{4,3,1,0,2:T(8,128)(2,1)} %bitcast.172, pred[8,4,96]{2,1,0:T(4,128)(4,1)S(1)} %broadcast_in_dim.66), kind=kLoop, calls=%fused_computation.10 | loop fusion | flops 3145728 | bytes 12585984 | tf_op jit(solution)/shard_map/jit(_take)/select_n | solution.py:83
  26.3 0.0 copy-start.10
  26.3 77.6 %all_to_all.30 = bf16[8,4,1,96,1024]{4,3,1,2,0:T(8,128)(2,1)S(1)} all-to-all(bf16[8,4,1,96,1024]{4,3,1,2,0:T(8,128)(2,1)S(1)} %select_bitcast_fusion), channel_id=1, replica_groups=mesh['dp'=2,'ep'=8] {'ep'}, dimensions={0} | all-to-all | bytes 12582912 | tf_op jit(solution)/shard_map/all_to_all | solution.py:84
  103.9 0.0 copy-start.2
  103.9 2.6 %copy-done.2 = bf16[8,4,1,96,1024]{4,3,1,2,0:T(8,128)(2,1)} copy-done((bf16[8,4,1,96,1024]{4,3,1,2,0:T(8,128)(2,1)}, bf16[8,4,1,96,1024]{4,3,1,2,0:T(8,128)(2,1)S(1)}, u32[]{:S(2)}) %copy-start.2) | copy-done | bytes 6291480
  106.5 0.0 copy-done.10
  106.5 5.2 %fusion = f32[4,8,96,512]{3,2,1,0:T(8,128)} fusion(bf16[8,4,1,96,1024]{4,3,1,2,0:T(8,128)(2,1)S(1)} %all_to_all.30, bf16[4,1024,512]{2,1,0:T(8,128)(2,1)S(1)} %copy-done.10), kind=kOutput, calls=%fused_computation.4 | convolution fusion | flops 3221225472 | bytes 16777216 | tf_op jit(solution)/shard_map/egcd,edf->egcf/dot_general | solution.py:57
  111.7 13.2 %convert_bitcast_fusion = bf16[1,4,8,96,1024]{4,3,2,1,0:T(8,128)(2,1)} fusion(bf16[4,512,1024]{2,1,0:T(8,128)(2,1)} %param.33, f32[4,8,96,512]{3,2,1,0:T(8,128)} %fusion, bf16[8,4,1,96,1024]{4,3,1,2,0:T(8,128)(2,1)} %copy-done.2, bf16[4,1024,512]{2,1,0:T(8,128)(2,1)} %param.31), kind=kOutput, calls=%fused_computation.8 | convolution fusion | flops 6455033856 | bytes 27262976 | tf_op jit(solution)/shard_map/egcf,efd->egcd/dot_general | solution.py:59
  124.9 6.6 %copy.45 = bf16[1,4,8,96,1024]{4,3,1,0,2:T(8,128)(2,1)} copy(bf16[1,4,8,96,1024]{4,3,2,1,0:T(8,128)(2,1)} %convert_bitcast_fusion) | data formatting | bytes 12582912 | tf_op jit(solution)/shard_map/broadcast_in_dim | solution.py:86
  131.5 0.0 copy-start.1
  131.5 0.0 copy-start.5
  131.5 5.2 %all-to-all-start.1 = ((bf16[1,4,8,96,1024]{4,3,1,0,2:T(8,128)(2,1)}), bf16[1,4,8,96,1024]{4,3,1,0,2:T(8,128)(2,1)}, u32[]{:S(2)}, u32[]{:S(2)}) async-start(bf16[1,4,8,96,1024]{4,3,1,0,2:T(8,128)(2,1)} %copy.45), calls=%async_computation.1 | async-start | bytes 12582912 | tf_op jit(solution)/shard_map/all_to_all | solution.py:86
  136.8 0.0 copy-done.6
  136.8 0.1 copy.39
  136.9 0.0 copy-done.7
  136.9 0.7 copy.41
  137.6 0.0 copy-done.8
  137.6 0.0 copy-done.9
  137.7 0.1 copy.40
  137.8 0.1 reshape.393
  137.9 0.0 copy-done.1
  137.9 0.1 fusion.37
  138.0 1.6 convolution_convert_fusion.1
  139.6 0.8 copy.35
  140.4 0.0 copy-done.5
  140.4 0.2 fusion.83
  140.5 7.0 %gather_fusion.2 = f32[1024]{0:T(1024)S(1)} fusion(f32[128,32]{0,1:T(8,128)S(1)} %fusion.83, s32[1024]{0:T(1024)S(1)} %reshape.393), kind=kCustom, calls=%fused_computation.2 | custom fusion | bytes 16384 | tf_op jit(solution)/shard_map/jit(take_along_axis)/gather | solution.py:52
  147.6 0.1 reshape.396
  147.7 1.5 copy.36
  149.2 3.9 %copy.37 = bf16[1024,1024]{0,1:T(8,128)(2,1)} copy(bf16[1024,1024]{1,0:T(8,128)(2,1)} %param.21) | data formatting | bytes 4194304 | tf_op args[4]
  153.2 0.1 fusion.78
  153.3 0.2 fusion.63
  153.5 0.0 slice-start
  153.5 0.5 convolution_bitcast_fusion.3
  154.0 0.1 fusion.65
  154.1 2.7 %convolution_bitcast_fusion.2 = f32[1,128,16,64]{1,3,2,0:T(8,128)S(1)} fusion(bf16[16,64,1024]{2,1,0:T(8,128)(2,1)} %bitcast.175, bf16[1,128,1024]{2,1,0:T(8,128)(2,1)S(1)} %copy-done.1, f32[1024]{0:T(1024)S(1)} %convert_element_type.78, f32[128]{0:T(128)S(1)} %add_rsqrt_fusion.2), kind=kOutput, calls=%fused_computation.27 | convolution fusion | flops 268959744 | bytes 2888192 | tf_op jit(solution)/shard_map/bsd,de->bse/dot_general | solution.py:35
  156.9 0.0 copy-start.3
  156.9 0.1 subtract_convert_fusion
  157.0 0.4 fusion.82
  157.4 0.0 slice-start.1
  157.4 0.2 fusion.31
  157.6 0.0 copy-done.4
  157.6 0.3 convolution_convert_fusion
  157.9 0.0 copy-done
  157.9 0.6 multiply_reduce_fusion.1
  158.5 0.0 copy-done.3
  158.5 0.1 fusion.62
  158.7 0.0 slice-done
  158.7 0.9 slice-done.1
  159.6 2.7 %fusion.44 = f32[128,4096]{1,0:T(8,128)} fusion(bf16[1024,4096]{1,0:T(8,128)(2,1)S(1)} %bitcast.174, f32[1,128,1024]{2,1,0:T(8,128)S(1)} %get-tuple-element.14, f32[1024]{0:T(1024)S(1)} %convert_element_type.87, f32[128]{0:T(128)S(1)} %add_rsqrt_fusion.1), kind=kOutput, calls=%fused_computation.56 | convolution fusion | flops 1074135040 | bytes 11014656 | tf_op jit(solution)/shard_map/bsd,df->bsf/dot_general | solution.py:46
  162.3 46.3 %all-to-all-done.1 = bf16[1,4,8,96,1024]{4,3,1,0,2:T(8,128)(2,1)} async-done(((bf16[1,4,8,96,1024]{4,3,1,0,2:T(8,128)(2,1)}), bf16[1,4,8,96,1024]{4,3,1,0,2:T(8,128)(2,1)}, u32[]{:S(2)}, u32[]{:S(2)}) %all-to-all-start.1) | async-done | bytes 6291488 | tf_op jit(solution)/shard_map/all_to_all | solution.py:86
  208.5 9.6 %gather_fusion.1 = bf16[1024,1024]{1,0:T(8,128)(2,1)} fusion(bf16[3072,1024]{1,0:T(8,128)(2,1)} %bitcast.48, s32[1024]{0:T(1024)S(1)} %broadcast_clamp_fusion), kind=kCustom, calls=%fused_computation.1 | custom fusion | bytes 4198400 | tf_op jit(solution)/shard_map/jit(_take)/gather | solution.py:87
  218.2 3.1 %multiply_reduce_fusion = f32[128,1024]{1,0:T(8,128)S(1)} fusion(bf16[1024,1024]{1,0:T(8,128)(2,1)} %gather_fusion.1, f32[128,8]{1,0:T(8,128)S(1)} %fusion.62, pred[128,8]{1,0:T(8,128)(4,1)S(1)} %compare_and_fusion), kind=kLoop, calls=%fused_computation.19 | loop fusion | flops 4063232 | bytes 2626560 | tf_op jit(solution)/shard_map/reduce_sum | solution.py:88
  221.3 9.9 %fusion.27 = bf16[1,128,1024]{2,1,0:T(8,128)(2,1)} fusion(f32[1,128,1024]{2,1,0:T(8,128)S(1)} %get-tuple-element.14, bf16[4096,1024]{1,0:T(8,128)(2,1)} %param.28, bf16[1024,4096]{1,0:T(8,128)(2,1)} %param.27, f32[128,4096]{1,0:T(8,128)} %fusion.44, f32[128,1024]{1,0:T(8,128)S(1)} %multiply_reduce_fusion, f32[1024]{0:T(1024)S(1)} %convert_element_type.87, ...), kind=kOutput, calls=%fused_computation.31 | convolution fusion | flops 2151415808 | bytes 20189696 | tf_op jit(solution)/shard_map/bsf,fd->bsd/dot_general | solution.py:47
  (22 shorter events, 0.2 us)
Async XLA Ops:
  0.0 157.9 %copy-start = (bf16[16,64,1024]{2,1,0:T(8,128)(2,1)S(1)}, bf16[16,64,1024]{2,1,0:T(8,128)(2,1)}, u32[]{:S(2)}) copy-start(bf16[16,64,1024]{2,1,0:T(8,128)(2,1)} %param.24) | copy-start | bytes 6291460
  26.3 80.2 %copy-start.10 = (bf16[4,1024,512]{2,1,0:T(8,128)(2,1)S(1)}, bf16[4,1024,512]{2,1,0:T(8,128)(2,1)}, u32[]{:S(2)}) copy-start(bf16[4,1024,512]{2,1,0:T(8,128)(2,1)} %param.32) | copy-start | bytes 12582916
  103.9 2.6 %copy-start.2 = (bf16[8,4,1,96,1024]{4,3,1,2,0:T(8,128)(2,1)}, bf16[8,4,1,96,1024]{4,3,1,2,0:T(8,128)(2,1)S(1)}, u32[]{:S(2)}) copy-start(bf16[8,4,1,96,1024]{4,3,1,2,0:T(8,128)(2,1)S(1)} %all_to_all.30) | copy-start | bytes 18874372
  131.5 5.3 %copy-start.6 = (s32[1,128,8]{1,2,0:T(8,128)S(1)}, s32[1,128,8]{1,2,0:T(8,128)}, u32[]{:S(2)}) copy-start(s32[1,128,8]{1,2,0:T(8,128)} %param.18) | copy-start | bytes 12292
  131.5 5.4 %copy-start.7 = (s32[1,128,8]{1,2,0:T(8,128)S(1)}, s32[1,128,8]{1,2,0:T(8,128)}, u32[]{:S(2)}) copy-start(s32[1,128,8]{1,2,0:T(8,128)} %param.19) | copy-start | bytes 12292
  131.5 6.1 %copy-start.8 = (bf16[1024]{0:T(1024)(128)(2,1)S(1)}, bf16[1024]{0:T(1024)(128)(2,1)}, u32[]{:S(2)}) copy-start(bf16[1024]{0:T(1024)(128)(2,1)} %param.20) | copy-start | bytes 6148
  131.5 6.1 %copy-start.9 = (bf16[1024]{0:T(1024)(128)(2,1)S(1)}, bf16[1024]{0:T(1024)(128)(2,1)}, u32[]{:S(2)}) copy-start(bf16[1024]{0:T(1024)(128)(2,1)} %param.25) | copy-start | bytes 6148
  131.5 6.3 %copy-start.1 = (bf16[1,128,1024]{2,1,0:T(8,128)(2,1)S(1)}, bf16[1,128,1024]{2,1,0:T(8,128)(2,1)}, u32[]{:S(2)}) copy-start(bf16[1,128,1024]{2,1,0:T(8,128)(2,1)} %param.17) | copy-start | bytes 786436
  131.5 8.8 %copy-start.5 = (bf16[1024,32]{0,1:T(8,128)(2,1)S(1)}, bf16[1024,32]{0,1:T(8,128)(2,1)}, u32[]{:S(2)}) copy-start(bf16[1024,32]{0,1:T(8,128)(2,1)} %param.30) | copy-start | bytes 196612
  131.5 77.0 %all-to-all-start.1 = ((bf16[1,4,8,96,1024]{4,3,1,0,2:T(8,128)(2,1)}), bf16[1,4,8,96,1024]{4,3,1,0,2:T(8,128)(2,1)}, u32[]{:S(2)}, u32[]{:S(2)}) async-start(bf16[1,4,8,96,1024]{4,3,1,0,2:T(8,128)(2,1)} %copy.45), calls=%async_computation.1 | async-start | bytes 12582912 | tf_op jit(solution)/shard_map/all_to_all | solution.py:86
  153.1 4.5 %copy-start.4 = (bf16[128,512]{0,1:T(8,128)(2,1)S(1)}, bf16[128,512]{0,1:T(8,128)(2,1)}, u32[]{:S(2)}) copy-start(bf16[128,512]{0,1:T(8,128)(2,1)} %copy.35) | copy-start | bytes 393220
  153.5 5.2 %slice-start = ((s8[8388608]{0:T(1024)(128)(4,1)}), s8[4194304]{0:T(1024)(128)(4,1)S(1)}, s32[]{:S(2)}) async-start(s8[8388608]{0:T(1024)(128)(4,1)} %bitcast.173), calls=%async_computation.2 | async-start | bytes 8388608
  156.9 1.6 copy-start.3
  157.4 2.2 slice-start.1
where the time goes:
time: 232 us; the launch traced here: 231 us
  blocking collectives  77.6 us (33%)
  local copies, waits for them, and re-layouts  52.7 us (23%)
  waiting for transfers between devices  46.3 us (20%)
  matrix products  37.2 us (16%)
  other arithmetic  11.8 us (5%)
  starting transfers between devices  5.25 us (2%)
    all_to_all x1, blocking collectives, per_device(): recv_buf = lax.all_to_all(send_buf, 'ep', 0, 1)  77.6 us
    all_to_all x1, waiting for transfers between devices, per_device(): lax.all_to_all(expert_out, 'ep', 1, 0)  46.3 us
    gather x1, local copies, waits for them, and re-layouts, per_device(): jnp.take(padded, owner_tok, axis=0)  14 us
    dot_general x1, matrix products, expert_ffn(): jnp.einsum('egcf,efd->egcd', hidden_act, exp_down, preferred_element_type...  13.2 us
    dot_general x1, matrix products, dense_branch(): jnp.einsum('bsf,fd->bsd', hidden_act, ffn_down, preferred_element_type=jn...  9.87 us
    unnamed x30, local copies, waits for them, and re-layouts  9.83 us
    gather x1, local copies, waits for them, and re-layouts, per_device(): jnp.take(back_buf, buf_pos.reshape(-1), axis=0)  9.63 us
    gather x4, local copies, waits for them, and re-layouts, route_gates(): jnp.take_along_axis(logits, choice_ids, axis=-1)  7.31 us
  transfers between devices with their start and end apart: 1, of which 1 were waited for; matrix products, arithmetic and copies ran while one was open for 11% of the time, Pallas kernels for 0%

commit v1 on v0

v1 whole, which is shorter than its diff:
```python
import functools

import jax
import jax.numpy as jnp
import numpy as np
from jax import lax
from jax.experimental import pallas as pl
from jax.experimental.pallas import tpu as pltpu
from jax.sharding import PartitionSpec as P

RMS_EPS = 1e-6
ROPE_BASE = 10000.0
MESH = pl.DeviceIdType.MESH
F32, BF16 = jnp.float32, jnp.bfloat16
LANES = 128
FF_BLOCK = 512
COL = 256


def rms_rows(row_vals, norm_scale):
    as_float = row_vals.astype(F32)
    inv_rms = lax.rsqrt(jnp.mean(as_float * as_float, axis=-1, keepdims=True) + RMS_EPS)
    return (as_float * inv_rms * norm_scale.astype(F32)).astype(BF16)


def silu(z):
    return z / (1.0 + jnp.exp(-z))


def dot(a, b):
    return jnp.dot(a, b, preferred_element_type=F32)


def rope_tables(seq_len, head_dim):
    half = head_dim // 2
    lane = np.arange(LANES)
    freq = ROPE_BASE ** (-2.0 * (lane % half) / head_dim)
    angle = np.arange(seq_len)[:, None] * freq[None, :]
    sign = np.where(lane % head_dim < half, -1.0, 1.0)
    return np.cos(angle).astype(np.float32), (np.sin(angle) * sign[None, :]).astype(np.float32)


def kernel(group, hidden, ids, attn_norm, w_query, w_key, w_value, w_out, ffn_norm, ffn_gate, ffn_up, ffn_down,
           moe_norm, w_router, exp_gate, exp_up, exp_down, cos_t, sin_t, out,
           v_hid, v_ids, v_an, v_wq, v_wk, v_wv, v_wo, v_fn, v_fg, v_fu, v_fd, v_mn, v_wr, v_eg, v_eu, v_ed, v_cos, v_sin,
           v_out, x_buf, g_buf, p_buf, pr_buf, tb, rb, qf, kf, vf, ctx, hb, att, ffn_acc,
           w_sem, s_sem, r_sem):
    tokens, model = v_hid.shape
    half = tokens // 2
    n_local = v_eg.shape[0]
    exp_ff = v_eg.shape[2]
    ff_dim = v_fg.shape[1]
    me = lax.axis_index('ep')
    partner = me + 1 - 2 * lax.rem(me, 2)
    right = lax.rem(me + 2, group)
    left = lax.rem(me + group - 2, group)

    loads = {}

    def load(name, src, dst):
        loads[name] = pltpu.make_async_copy(src, dst, w_sem.at[len(loads)])
        loads[name].start()

    def ready(*names):
        for name in names:
            loads[name].wait()

    copies = {}

    def remote(name, src, dst, device):
        k = len(copies)
        copies[name] = pltpu.make_async_remote_copy(
            src_ref=src, dst_ref=dst, send_sem=s_sem.at[k], recv_sem=r_sem.at[k],
            device_id={'ep': device}, device_id_type=MESH)
        return copies[name]

    def send(*names):
        for name in names:
            copies[name].start()

    def recv(*names):
        for name in names:
            copies[name].wait_recv()

    lo, hi, al, ot = pl.ds(0, half), pl.ds(half, half), pl.ds(0, tokens), pl.ds(tokens, tokens)
    remote('a1', x_buf.at[0, lo], x_buf.at[1, lo], right)
    remote('a2', x_buf.at[0, hi], x_buf.at[1, hi], left)
    remote('a3', x_buf.at[0, hi], x_buf.at[2, hi], right)
    remote('a4', x_buf.at[0, lo], x_buf.at[2, lo], left)
    remote('f1', x_buf.at[1, lo], x_buf.at[3, lo], right)
    remote('f2', x_buf.at[1, hi], x_buf.at[3, hi], left)
    for c in range(4):
        remote(f'd{c}', x_buf.at[c, al], x_buf.at[c, ot], partner)
    remote('g1', g_buf.at[0, 0], g_buf.at[1, 0], right)
    remote('g2', g_buf.at[0, 0], g_buf.at[2, 0], left)
    remote('g3', g_buf.at[1, 0], g_buf.at[3, 0], right)
    for c in range(4):
        remote(f'gd{c}', g_buf.at[c, 0], g_buf.at[c, 1], partner)
    for c in range(4):
        remote(f'p{c}', p_buf.at[c, ot], pr_buf.at[c], partner)
    remote('i1', p_buf.at[1, hi], rb.at[1, hi], right)
    remote('i2', p_buf.at[1, lo], rb.at[0, lo], left)
    remote('o1', p_buf.at[3, lo], tb.at[lo], right)
    remote('o2', p_buf.at[3, hi], tb.at[hi], left)
    remote('w1', p_buf.at[2, lo], rb.at[1, lo], right)
    remote('w2', p_buf.at[2, hi], rb.at[0, hi], left)

    load('hid', hidden, v_hid)
    load('mn', moe_norm, v_mn)
    load('wr', w_router, v_wr)
    load('ids', ids, v_ids)
    load('an', attn_norm, v_an)
    load('wq', w_query, v_wq)
    load('wk', w_key, v_wk)
    load('wv', w_value, v_wv)
    load('cos', cos_t, v_cos)
    load('sin', sin_t, v_sin)

    barrier = pltpu.get_barrier_semaphore()
    for peer in (partner, left, right):
        pl.semaphore_signal(barrier, inc=1, device_id={'ep': peer}, device_id_type=MESH)

    for e in range(n_local):
        load(f'eg{e}', exp_gate.at[e], v_eg.at[e])
        load(f'eu{e}', exp_up.at[e], v_eu.at[e])
        load(f'ed{e}', exp_down.at[e], v_ed.at[e])
    load('wo', w_out, v_wo)
    load('fn', ffn_norm, v_fn)

    ready('hid', 'mn')
    x_buf[0, :tokens] = rms_rows(v_hid[...], v_mn[...])
    pl.semaphore_wait(barrier, 3)
    send('a1', 'a2', 'a3', 'a4', 'd0')

    ready('wr', 'ids')
    logits = dot(x_buf[0, :tokens], v_wr[...])
    n_experts = logits.shape[1]
    chosen = lax.broadcasted_iota(jnp.int32, logits.shape, 1)
    mask = jnp.zeros(logits.shape, jnp.bool_)
    id_vals = v_ids[...]
    for j in range(id_vals.shape[1]):
        mask = jnp.logical_or(mask, chosen == id_vals[:, j:j + 1])
    top = jnp.max(jnp.where(mask, logits, -jnp.inf), axis=-1, keepdims=True)
    powers = jnp.where(mask, jnp.exp(logits - top), 0.0)
    gates = powers / jnp.sum(powers, axis=-1, keepdims=True)
    g_buf[0, 0] = gates.T
    send('g1', 'g2', 'gd0')

    ready('an', 'wq', 'wk', 'wv', 'cos', 'sin')
    normed = rms_rows(v_hid[...], v_an[...])
    qf[...] = dot(normed, v_wq[...])
    kf[...] = dot(normed, v_wk[...])
    vf[...] = dot(normed, v_wv[...])

    recv('a1', 'a2')
    send('f1', 'f2', 'd1')
    recv('g1', 'g2')
    send('g3', 'gd1', 'gd2')

    n_blk = ff_dim // 1024
    for b in range(n_blk):
        cols = pl.ds(b * 1024, 1024)
        load(f'fg{b}', ffn_gate.at[:, cols], v_fg.at[:, cols])
        load(f'fu{b}', ffn_up.at[:, cols], v_fu.at[:, cols])
        load(f'fd{b}', ffn_down.at[cols], v_fd.at[cols])

    lane = lax.broadcasted_iota(jnp.int32, (tokens, LANES), 1)
    low_half = lax.rem(lane, 64) < 32
    head0 = lane < 64
    cos_v, sin_v = v_cos[...], v_sin[...]

    def rope(x):
        swapped = jnp.where(low_half, pltpu.roll(x, LANES - 32, 1), pltpu.roll(x, 32, 1))
        return x * cos_v + swapped * sin_v

    row = lax.rem(lax.broadcasted_iota(jnp.int32, (2 * tokens, tokens), 0), tokens)
    causal = row >= lax.broadcasted_iota(jnp.int32, (2 * tokens, tokens), 1)
    for t in range(kf.shape[1] // LANES):
        kt = rope(kf[:, t * LANES:(t + 1) * LANES])
        vt = vf[:, t * LANES:(t + 1) * LANES]
        kt_r, vt_r = pltpu.roll(kt, 64, 1), pltpu.roll(vt, 64, 1)
        for s in range(2):
            g = 2 * t + s
            k2 = (jnp.where(head0, kt, kt_r) if s == 0 else jnp.where(head0, kt_r, kt)).astype(BF16)
            v2 = (jnp.where(head0, vt, vt_r) if s == 0 else jnp.where(head0, vt_r, vt)).astype(BF16)
            q = rope(qf[:, g * LANES:(g + 1) * LANES])
            q2 = jnp.concatenate([jnp.where(head0, q, 0.0), jnp.where(head0, 0.0, q)], axis=0).astype(BF16)
            scores = lax.dot_general(q2, k2, (((1,), (1,)), ((), ())), preferred_element_type=F32) * 64 ** -0.5
            scores = jnp.where(causal, scores, -jnp.inf)
            prob = jnp.exp(scores - jnp.max(scores, axis=-1, keepdims=True))
            prob = (prob / jnp.sum(prob, axis=-1, keepdims=True)).astype(BF16)
            both = dot(prob, v2)
            ctx[:, g * LANES:(g + 1) * LANES] = jnp.where(head0, both[:tokens], both[tokens:]).astype(BF16)

    recv('a3', 'a4')
    send('d2')

    e_lane = lax.broadcasted_iota(jnp.int32, (2 * tokens, n_experts), 1) - me * n_local
    t_lane = lax.broadcasted_iota(jnp.int32, (n_experts, tokens), 1) < half

    def chunk_gates(c):
        parts = []
        for par in range(2):
            if c == 0:
                gt = g_buf[0, par]
            elif c == 3:
                gt = g_buf[3, par]
            elif c == 1:
                gt = jnp.where(t_lane, g_buf[1, par], g_buf[2, par])
            else:
                gt = jnp.where(t_lane, g_buf[2, par], g_buf[1, par])
            parts.append(gt.T)
        return jnp.concatenate(parts, axis=0)

    def expert(c, e, gates_c):
        gate = jnp.sum(jnp.where(e_lane == e, gates_c, 0.0), axis=-1, keepdims=True)
        used = gate > 0.0
        x = x_buf[c]
        for n in range(exp_ff // COL):
            cols = slice(n * COL, (n + 1) * COL)
            act = silu(dot(x, v_eg[e, :, cols])) * dot(x, v_eu[e, :, cols])
            hb[:, cols] = jnp.where(used, act, 0.0).astype(BF16)
        h = hb[...]
        for n in range(model // COL):
            cols = slice(n * COL, (n + 1) * COL)
            y = gate * dot(h, v_ed[e, :, cols]).astype(BF16).astype(F32)
            p_buf[c, :, cols] = y if e == 0 else p_buf[c, :, cols] + y

    def ffn_block(b, x):
        act_cols = slice(b * FF_BLOCK, (b + 1) * FF_BLOCK)
        for n in range(FF_BLOCK // COL):
            cols = slice(b * FF_BLOCK + n * COL, b * FF_BLOCK + (n + 1) * COL)
            act = silu(dot(x, v_fg[:, cols])) * dot(x, v_fu[:, cols])
            hb[:tokens, n * COL:(n + 1) * COL] = act.astype(BF16)
        h = hb[:tokens]
        for n in range(model // COL):
            cols = slice(n * COL, (n + 1) * COL)
            y = dot(h, v_fd[act_cols, cols])
            ffn_acc[:, cols] = y + (att[:, cols].astype(F32) if b == 0 else ffn_acc[:, cols])

    def add_partner(c):
        recv(f'p{c}')
        p_buf[c, :tokens] = p_buf[c, :tokens] + pr_buf[c]

    for e in range(n_local):
        ready(f'eg{e}', f'eu{e}', f'ed{e}')

    recv('d1', 'gd1', 'gd2')
    g = chunk_gates(1)
    expert(1, 0, g)
    expert(1, 1, g)
    recv('f1', 'f2', 'g3')
    send('d3', 'gd3')
    expert(1, 2, g)
    expert(1, 3, g)
    send('p1')
    recv('d3', 'gd3')
    g = chunk_gates(3)
    expert(3, 0, g)
    expert(3, 1, g)
    add_partner(1)
    send('i1', 'i2')
    expert(3, 2, g)
    expert(3, 3, g)
    send('p3')
    recv('d2')
    g = chunk_gates(2)
    expert(2, 0, g)
    expert(2, 1, g)
    add_partner(3)
    send('o1', 'o2')
    expert(2, 2, g)
    expert(2, 3, g)
    send('p2')
    recv('d0', 'gd0')
    g = chunk_gates(0)
    expert(0, 0, g)
    expert(0, 1, g)
    add_partner(2)
    expert(0, 2, g)
    expert(0, 3, g)
    send('p0')

    ready('wo', 'fn')
    att[...] = (v_hid[...].astype(F32) + dot(ctx[...], v_wo[...])).astype(BF16)
    normed_ffn = rms_rows(att[...], v_fn[...])
    for b in range(ff_dim // FF_BLOCK):
        if (b * FF_BLOCK) % 1024 == 0:
            i = b * FF_BLOCK // 1024
            ready(f'fg{i}', f'fu{i}', f'fd{i}')
        ffn_block(b, normed_ffn)
        if b == 2:
            recv('o1')
            p_buf[2, :half] = p_buf[2, :half] + tb[:half]
            send('w1')
            recv('o2')
            p_buf[2, half:tokens] = p_buf[2, half:tokens] + tb[half:]
            send('w2')
    add_partner(0)
    ffn_acc[...] = ffn_acc[...] + p_buf[0, :tokens]
    recv('i1', 'i2', 'w1', 'w2')
    v_out[...] = (ffn_acc[...] + rb[0] + rb[1]).astype(BF16)
    done = pltpu.make_async_copy(v_out, out, w_sem.at[len(loads)])
    done.start()
    for copy in copies.values():
        copy.wait_send()
    done.wait()


def solution(mesh):
    group = mesh.shape['ep']
    row_spec = P(('dp', 'ep'), None, None)
    vec_spec = P(None)
    mat_spec = P(None, None)
    cube_spec = P(None, None, None)
    expert_spec = P('ep', None, None)

    def per_device(hidden, expert_ids, slot_ids, attn_norm, w_query, w_key, w_value, w_out, ffn_norm, ffn_gate, ffn_up, ffn_down, moe_norm, w_router, exp_gate, exp_up, exp_down):
        n_seqs, seq_len, model = hidden.shape
        tokens = n_seqs * seq_len
        n_heads, head_dim = w_out.shape[0], w_out.shape[1]
        top_k = expert_ids.shape[-1]
        n_local, _, exp_ff = exp_gate.shape
        n_experts = w_router.shape[1]
        kv_dim = w_key.shape[1]
        assert n_seqs == 1 and group == 8 and head_dim == 64
        cos_t, sin_t = rope_tables(seq_len, head_dim)
        args = (hidden.reshape(tokens, model), expert_ids.reshape(tokens, top_k), attn_norm.reshape(1, model),
                w_query, w_key, w_value, w_out.reshape(n_heads * head_dim, model), ffn_norm.reshape(1, model),
                ffn_gate, ffn_up, ffn_down, moe_norm.reshape(1, model), w_router, exp_gate, exp_up, exp_down,
                jnp.asarray(cos_t), jnp.asarray(sin_t))
        vmem = [pltpu.VMEM(a.shape, a.dtype) for a in args]
        scratch = vmem + [
            pltpu.VMEM((tokens, model), BF16),
            pltpu.VMEM((4, 2 * tokens, model), BF16),
            pltpu.VMEM((4, 2, n_experts, tokens), F32),
            pltpu.VMEM((4, 2 * tokens, model), F32),
            pltpu.VMEM((4, tokens, model), F32),
            pltpu.VMEM((tokens, model), F32),
            pltpu.VMEM((2, tokens, model), F32),
            pltpu.VMEM((tokens, n_heads * head_dim), F32),
            pltpu.VMEM((tokens, kv_dim), F32),
            pltpu.VMEM((tokens, kv_dim), F32),
            pltpu.VMEM((tokens, n_heads * head_dim), BF16),
            pltpu.VMEM((2 * tokens, exp_ff), BF16),
            pltpu.VMEM((tokens, model), BF16),
            pltpu.VMEM((tokens, model), F32),
            pltpu.SemaphoreType.DMA((48,)),
            pltpu.SemaphoreType.DMA((28,)),
            pltpu.SemaphoreType.DMA((28,)),
        ]
        result = pl.pallas_call(
            functools.partial(kernel, group),
            out_shape=jax.ShapeDtypeStruct((tokens, model), BF16),
            in_specs=[pl.BlockSpec(memory_space=pl.ANY)] * len(args),
            out_specs=pl.BlockSpec(memory_space=pl.ANY),
            scratch_shapes=scratch,
            compiler_params=pltpu.CompilerParams(collective_id=0, has_side_effects=True, vmem_limit_bytes=67043328),
        )(*args)
        return result.reshape(n_seqs, seq_len, model)

    return jax.shard_map(per_device, mesh=mesh, in_specs=(row_spec, row_spec, row_spec, vec_spec, mat_spec, mat_spec, mat_spec, cube_spec, vec_spec, mat_spec, mat_spec, mat_spec, vec_spec, mat_spec, expert_spec, expert_spec, expert_spec), out_specs=row_spec, check_vma=False)
```

time: 232 us -> 51.3 us (0.22)
  blocking collectives: 77.6 us -> 0 us
  waiting for transfers between devices: 46.3 us -> 0 us
  local copies, waits for them, and re-layouts: 52.7 us -> 8.57 us
  Pallas kernels: 0 us -> 42.5 us
  matrix products: 37.2 us -> 0 us
  other arithmetic: 11.8 us -> 0 us
  starting transfers between devices: 5.25 us -> 0 us
    all_to_all x1 -> x0, blocking collectives: 77.6 us -> none  [per_device(): recv_buf = lax.all_to_all(send_buf, 'ep', 0, 1)]
    all_to_all x1 -> x0, waiting for transfers between devices: 46.3 us -> none  [per_device(): lax.all_to_all(expert_out, 'ep', 1, 0)]
    pallas_call x0 -> x1, Pallas kernels: none -> 42.5 us  [per_device(): pl.pallas_call(functools.partial(kernel, group), out_shape=jax.ShapeDtype...]
    dot_general x11 -> x0, matrix products: 37.2 us -> none  [the longest x1 13.2 us: expert_ffn(): jnp.einsum('egcf,efd->egcd', hidden_act, exp_down, preferred_element_type...]
    gather x6 -> x0, local copies, waits for them, and re-layouts: 30.9 us -> none  [the longest x1 14 us: per_device(): jnp.take(padded, owner_tok, axis=0)]
    broadcast_in_dim x2 -> x0, local copies, waits for them, and re-layouts: 6.68 us -> none  [the longest x1 6.59 us: per_device(): lax.all_to_all(expert_out, 'ep', 1, 0)]
    all_to_all x1 -> x0, starting transfers between devices: 5.25 us -> none  [per_device(): lax.all_to_all(expert_out, 'ep', 1, 0)]
    unnamed x30 -> x3, local copies, waits for them, and re-layouts: 9.83 us -> 4.75 us
  transfers between devices with their start and end apart: 1 -> 0, of which waited for: 1 -> 0; matrix products, arithmetic and copies ran while one was open for 11% -> 0% of each run, Pallas kernels for 0% -> 0%
where the time goes in v1:
time: 51.3 us; the launch traced here: 51 us
  Pallas kernels  42.5 us (83%)
  local copies, waits for them, and re-layouts  8.57 us (17%)
    pallas_call x1, Pallas kernels, per_device(): pl.pallas_call(functools.partial(kernel, group), out_shape=jax.ShapeDtype...  42.5 us
    unnamed x3, local copies, waits for them, and re-layouts  4.75 us
    reshape x1, local copies, waits for them, and re-layouts, per_device(): attn_norm.reshape(1, model)  1.28 us
    reshape x1, local copies, waits for them, and re-layouts, per_device(): ffn_norm.reshape(1, model)  1.27 us
    reshape x1, local copies, waits for them, and re-layouts, per_device(): moe_norm.reshape(1, model)  1.27 us

profile of v1, /device:TPU:112, one launch (start us, length us, event | category | flops | bytes accessed | tf_op | source)
XLA Modules:
  0.0 51.0 jit_solution(7663089718881291332)
XLA Ops:
  0.0 1.3 %reshape.23.attn_norm = bf16[1,1024]{1,0:T(2,128)(2,1)} reshape(bf16[1024]{0:T(1024)(128)(2,1)} %param.21) | data formatting | bytes 4096 | tf_op jit(solution)/shard_map/reshape | solution.py:328
  1.3 1.3 %reshape.25.ffn_norm = bf16[1,1024]{1,0:T(2,128)(2,1)} reshape(bf16[1024]{0:T(1024)(128)(2,1)} %param.26) | data formatting | bytes 4096 | tf_op jit(solution)/shard_map/reshape | solution.py:329
  2.6 1.3 %reshape.26.moe_norm = bf16[1,1024]{1,0:T(2,128)(2,1)} reshape(bf16[1024]{0:T(1024)(128)(2,1)} %param.30) | data formatting | bytes 4096 | tf_op jit(solution)/shard_map/reshape | solution.py:330
  3.8 1.4 %copy.19 = s32[1,128,8]{2,1,0:T(8,128)} copy(s32[1,128,8]{1,2,0:T(8,128)} %param.20) | data formatting | bytes 8192 | tf_op args[1]
  5.2 1.7 %copy.20.w_router = bf16[1024,32]{1,0:T(8,128)(2,1)} copy(bf16[1024,32]{0,1:T(8,128)(2,1)} %param.31) | data formatting | bytes 131072 | tf_op args[13]
  6.9 42.5 %shard_map.172 = bf16[128,1024]{1,0:T(8,128)(2,1)} custom-call(bf16[128,1024]{1,0:T(8,128)(2,1)} %bitcast.6, s32[128,8]{1,0:T(8,128)} %bitcast.7, bf16[1,1024]{1,0:T(2,128)(2,1)} %reshape.23.attn_norm, bf16[1024,1024]{1,0:T(8,128)(2,1)} %w_query.1, bf16[1024,512]{1,0:T(8,128)(2,1)} %w_key.1, bf16[1024,512]{1,0:T(8,128)(2,1)} %w_value.1, ...), custom_call_target="tpu_custom_call" | custom-call | tf_op jit(solution)/shard_map/pallas_call | solution.py:352
  49.4 1.7 %copy.22 = bf16[1,128,1024]{2,1,0:T(8,128)(2,1)} copy(bf16[1,128,1024]{2,1,0:T(8,128)(2,1)} %bitcast.5) | data formatting | bytes 524288

commit v2 on v1

v2 whole, which is shorter than its diff:
```python
import functools

import jax
import jax.numpy as jnp
import numpy as np
from jax import lax
from jax.experimental import pallas as pl
from jax.experimental.pallas import tpu as pltpu
from jax.sharding import PartitionSpec as P

RMS_EPS = 1e-6
ROPE_BASE = 10000.0
MESH = pl.DeviceIdType.MESH
F32, BF16 = jnp.float32, jnp.bfloat16
LANES = 128
FF_BLOCK = 512
COL = 256
N_P = 2
N_O = 4


def rms_rows(row_vals, norm_scale):
    as_float = row_vals.astype(F32)
    inv_rms = lax.rsqrt(jnp.mean(as_float * as_float, axis=-1, keepdims=True) + RMS_EPS)
    return (as_float * inv_rms * norm_scale).astype(BF16)


def silu(z):
    return z / (1.0 + jnp.exp(-z))


def dot(a, b):
    return jnp.dot(a, b, preferred_element_type=F32)


def rope_tables(seq_len, head_dim):
    half = head_dim // 2
    lane = np.arange(LANES)
    freq = ROPE_BASE ** (-2.0 * (lane % half) / head_dim)
    angle = np.arange(seq_len)[:, None] * freq[None, :]
    sign = np.where(lane % head_dim < half, -1.0, 1.0)
    return np.cos(angle).astype(np.float32), (np.sin(angle) * sign[None, :]).astype(np.float32)


def kernel(group, hidden, ids, attn_norm, w_query, w_key, w_value, w_out, ffn_norm, ffn_gate, ffn_up, ffn_down,
           moe_norm, w_router, exp_gate, exp_up, exp_down, cos_t, sin_t, out,
           v_hid, v_ids, v_an, v_wq, v_wk, v_wv, v_wo, v_fn, v_fg, v_fu, v_fd, v_mn, v_wr, v_eg, v_eu, v_ed, v_cos, v_sin,
           v_out, x_buf, g_buf, p_buf, pr_buf, tb, rb, qf, kf, vf, ctx, hb, gate_b, att, ffn_acc,
           w_sem, s_sem, r_sem):
    tokens, model = v_hid.shape
    half, quarter = tokens // 2, tokens // 4
    n_local = v_eg.shape[0]
    exp_ff = v_eg.shape[2]
    ff_dim = v_fg.shape[1]
    n_experts = v_wr.shape[0]
    me = lax.axis_index('ep')
    partner = me + 1 - 2 * lax.rem(me, 2)
    right = lax.rem(me + 2, group)
    left = lax.rem(me + group - 2, group)

    loads = {}

    def load(name, src, dst):
        loads[name] = pltpu.make_async_copy(src, dst, w_sem.at[len(loads)])
        loads[name].start()

    def ready(*names):
        for name in names:
            loads[name].wait()

    copies = {}

    def remote(name, src, dst, device):
        k = len(copies)
        copies[name] = pltpu.make_async_remote_copy(
            src_ref=src, dst_ref=dst, send_sem=s_sem.at[k], recv_sem=r_sem.at[k],
            device_id={'ep': device}, device_id_type=MESH)

    def send(*names):
        for name in names:
            copies[name].start()

    def recv(*names):
        for name in names:
            copies[name].wait_recv()

    lo, hi, al, ot = pl.ds(0, half), pl.ds(half, half), pl.ds(0, tokens), pl.ds(tokens, tokens)
    q0, q1, q2, q3 = (pl.ds(i * quarter, quarter) for i in range(4))
    p_cols = [pl.ds(n * model // N_P, model // N_P) for n in range(N_P)]
    o_cols = [pl.ds(n * model // N_O, model // N_O) for n in range(N_O)]
    for name, c_src, rows, c_dst, device in (
            ('a1a', 0, q0, 1, right), ('a1b', 0, q1, 1, right), ('a2a', 0, q2, 1, left), ('a2b', 0, q3, 1, left),
            ('a3a', 0, q2, 2, right), ('a3b', 0, q3, 2, right), ('a4a', 0, q0, 2, left), ('a4b', 0, q1, 2, left),
            ('f1a', 1, q0, 3, right), ('f1b', 1, q1, 3, right), ('f2a', 1, q2, 3, left), ('f2b', 1, q3, 3, left)):
        remote(name, x_buf.at[c_src, rows], x_buf.at[c_dst, rows], device)
    for c in range(4):
        remote(f'd{c}', x_buf.at[c, al], x_buf.at[c, ot], partner)
    remote('g1', g_buf.at[0, 0], g_buf.at[1, 0], right)
    remote('g2', g_buf.at[0, 0], g_buf.at[2, 0], left)
    remote('g3', g_buf.at[1, 0], g_buf.at[3, 0], right)
    for c in range(4):
        remote(f'gd{c}', g_buf.at[c, 0], g_buf.at[c, 1], partner)
    for n, cols in enumerate(p_cols):
        for c in range(4):
            remote(f'p{c}_{n}', p_buf.at[c, ot, cols], pr_buf.at[c, :, cols], partner)
        remote(f'i1_{n}', p_buf.at[1, hi, cols], rb.at[1, hi, cols], right)
        remote(f'i2_{n}', p_buf.at[1, lo, cols], rb.at[0, lo, cols], left)
    for n, cols in enumerate(o_cols):
        remote(f'o1_{n}', p_buf.at[3, lo, cols], tb.at[lo, cols], right)
        remote(f'o2_{n}', p_buf.at[3, hi, cols], tb.at[hi, cols], left)
        remote(f'w1_{n}', p_buf.at[2, lo, cols], rb.at[1, lo, cols], right)
        remote(f'w2_{n}', p_buf.at[2, hi, cols], rb.at[0, hi, cols], left)

    load('hid', hidden, v_hid)
    load('mn', moe_norm, v_mn)
    load('wr', w_router, v_wr)
    load('ids', ids, v_ids)
    load('an', attn_norm, v_an)
    load('wq', w_query, v_wq)
    load('wk', w_key, v_wk)
    load('wv', w_value, v_wv)
    load('cos', cos_t, v_cos)
    load('sin', sin_t, v_sin)

    barrier = pltpu.get_barrier_semaphore()
    for peer in (partner, left, right):
        pl.semaphore_signal(barrier, inc=1, device_id={'ep': peer}, device_id_type=MESH)

    load('wo', w_out, v_wo)
    for e in range(n_local):
        load(f'eg{e}', exp_gate.at[e], v_eg.at[e])
        load(f'eu{e}', exp_up.at[e], v_eu.at[e])
    for e in range(n_local):
        load(f'ed{e}', exp_down.at[e], v_ed.at[e])
    load('fn', ffn_norm, v_fn)

    def norm_row(ref):
        scale = ref[...].astype(F32)
        return jnp.concatenate([scale[r:r + 1] for r in range(scale.shape[0])], axis=1)

    ready('hid', 'mn')
    x_buf[0, :tokens] = rms_rows(v_hid[...], norm_row(v_mn))
    pl.semaphore_wait(barrier, 3)
    send('a1a', 'a2a', 'a1b', 'a2b', 'd0')

    ready('wr', 'ids')
    logits = lax.dot_general(v_wr[...], x_buf[0, :tokens], (((1,), (1,)), ((), ())), preferred_element_type=F32)
    expert_row = lax.broadcasted_iota(jnp.int32, logits.shape, 0)
    id_vals = v_ids[...]
    mask = expert_row == id_vals[0:1]
    for j in range(1, id_vals.shape[0]):
        mask = jnp.logical_or(mask, expert_row == id_vals[j:j + 1])
    top = jnp.max(jnp.where(mask, logits, -jnp.inf), axis=0, keepdims=True)
    powers = jnp.where(mask, jnp.exp(logits - top), 0.0)
    g_buf[0, 0] = powers / jnp.sum(powers, axis=0, keepdims=True)
    send('g1', 'g2', 'gd0', 'a3a', 'a4a')

    ready('an', 'wq', 'wk', 'wv', 'cos', 'sin')
    normed = rms_rows(v_hid[...], norm_row(v_an))
    qf[...] = dot(normed, v_wq[...])
    kf[...] = dot(normed, v_wk[...])
    vf[...] = dot(normed, v_wv[...])

    lane = lax.broadcasted_iota(jnp.int32, (tokens, LANES), 1)
    low_half = lax.rem(lane, 64) < 32
    head0 = lane < 64
    row = lax.rem(lax.broadcasted_iota(jnp.int32, (2 * tokens, tokens), 0), tokens)
    causal = row >= lax.broadcasted_iota(jnp.int32, (2 * tokens, tokens), 1)

    def rope(x):
        swapped = jnp.where(low_half, pltpu.roll(x, LANES - 32, 1), pltpu.roll(x, 32, 1))
        return x * v_cos[...] + swapped * v_sin[...]

    def attend(t):
        kt = rope(kf[:, t * LANES:(t + 1) * LANES])
        vt = vf[:, t * LANES:(t + 1) * LANES]
        kt_r, vt_r = pltpu.roll(kt, 64, 1), pltpu.roll(vt, 64, 1)
        for s in range(2):
            g = 2 * t + s
            k2 = (jnp.where(head0, kt, kt_r) if s == 0 else jnp.where(head0, kt_r, kt)).astype(BF16)
            v2 = (jnp.where(head0, vt, vt_r) if s == 0 else jnp.where(head0, vt_r, vt)).astype(BF16)
            q = rope(qf[:, g * LANES:(g + 1) * LANES])
            q2 = jnp.concatenate([jnp.where(head0, q, 0.0), jnp.where(head0, 0.0, q)], axis=0).astype(BF16)
            scores = lax.dot_general(q2, k2, (((1,), (1,)), ((), ())), preferred_element_type=F32) * 64 ** -0.5
            scores = jnp.where(causal, scores, -jnp.inf)
            prob = jnp.exp(scores - jnp.max(scores, axis=-1, keepdims=True))
            prob = (prob / jnp.sum(prob, axis=-1, keepdims=True)).astype(BF16)
            both = dot(prob, v2)
            ctx[:, g * LANES:(g + 1) * LANES] = jnp.where(head0, both[:tokens], both[tokens:]).astype(BF16)

    e_lane = lax.broadcasted_iota(jnp.int32, (tokens, n_experts), 1) - me * n_local
    t_lane = lax.broadcasted_iota(jnp.int32, (n_experts, tokens), 1) < half

    def set_gates(c, par):
        if c == 0:
            gt = g_buf[0, par]
        elif c == 3:
            gt = g_buf[3, par]
        elif c == 1:
            gt = jnp.where(t_lane, g_buf[1, par], g_buf[2, par])
        else:
            gt = jnp.where(t_lane, g_buf[2, par], g_buf[1, par])
        gates_c = gt.T
        for e in range(n_local):
            gate = jnp.sum(jnp.where(e_lane == e, gates_c, 0.0), axis=-1, keepdims=True)
            gate_b[e, par * tokens:(par + 1) * tokens] = jnp.broadcast_to(gate, (tokens, LANES))

    def act(c, rows, e):
        x = x_buf[c, rows]
        used = gate_b[e, rows] > 0.0
        used = jnp.concatenate([used.astype(F32)] * (COL // LANES), axis=1) > 0.0
        for n in range(exp_ff // COL):
            cols = slice(n * COL, (n + 1) * COL)
            z = silu(dot(x, v_eg[e, :, cols])) * dot(x, v_eu[e, :, cols])
            hb[rows, e * exp_ff + n * COL:e * exp_ff + (n + 1) * COL] = jnp.where(used, z, 0.0).astype(BF16)

    def down(c):
        for n in range(model // COL):
            cols = slice(n * COL, (n + 1) * COL)
            for e in range(n_local):
                y = dot(hb[:, e * exp_ff:(e + 1) * exp_ff], v_ed[e, :, cols]).astype(BF16).astype(F32)
                y = y * jnp.concatenate([gate_b[e]] * (COL // LANES), axis=1)
                p_buf[c, :, cols] = y if e == 0 else p_buf[c, :, cols] + y
            if (n + 1) * COL % (model // N_P) == 0:
                send(f'p{c}_{((n + 1) * COL) // (model // N_P) - 1}')

    def add_partner(c, n):
        recv(f'p{c}_{n}')
        cols = slice(n * model // N_P, (n + 1) * model // N_P)
        p_buf[c, :tokens, cols] = p_buf[c, :tokens, cols] + pr_buf[c, :, cols]

    def send_near():
        for n in range(N_P):
            add_partner(1, n)
            send(f'i1_{n}', f'i2_{n}')

    def send_far():
        for n in range(N_P):
            add_partner(3, n)
            for k in range(n * N_O // N_P, (n + 1) * N_O // N_P):
                send(f'o1_{k}', f'o2_{k}')

    def pass_on(n):
        cols = slice(n * model // N_O, (n + 1) * model // N_O)
        recv(f'o1_{n}')
        p_buf[2, :half, cols] = p_buf[2, :half, cols] + tb[:half, cols]
        send(f'w1_{n}')
        recv(f'o2_{n}')
        p_buf[2, half:tokens, cols] = p_buf[2, half:tokens, cols] + tb[half:, cols]
        send(f'w2_{n}')

    def ffn_block(b, x):
        act_cols = slice(b * FF_BLOCK, (b + 1) * FF_BLOCK)
        for n in range(FF_BLOCK // COL):
            cols = slice(b * FF_BLOCK + n * COL, b * FF_BLOCK + (n + 1) * COL)
            z = silu(dot(x, v_fg[:, cols])) * dot(x, v_fu[:, cols])
            hb[:tokens, n * COL:(n + 1) * COL] = z.astype(BF16)
        h = hb[:tokens, :FF_BLOCK]
        for n in range(model // COL):
            cols = slice(n * COL, (n + 1) * COL)
            y = dot(h, v_fd[act_cols, cols])
            ffn_acc[:, cols] = y + (att[:, cols].astype(F32) if b == 0 else ffn_acc[:, cols])

    same, other, both = slice(0, tokens), slice(tokens, 2 * tokens), slice(0, 2 * tokens)

    attend(0)
    attend(1)
    attend(2)
    recv('a1a', 'a2a')
    send('f1a', 'f2a')
    attend(3)
    ready('wo', 'fn')
    att[...] = (v_hid[...].astype(F32) + dot(ctx[...], v_wo[...])).astype(BF16)
    recv('a1b', 'a2b')
    send('f1b', 'f2b', 'd1', 'a3b', 'a4b')
    recv('g1', 'g2')
    send('g3', 'gd1', 'gd2')

    n_blk = ff_dim // 1024
    for b in range(n_blk):
        cols = pl.ds(b * 1024, 1024)
        load(f'fg{b}', ffn_gate.at[:, cols], v_fg.at[:, cols])
        load(f'fu{b}', ffn_up.at[:, cols], v_fu.at[:, cols])
        load(f'fd{b}', ffn_down.at[cols], v_fd.at[cols])

    set_gates(1, 0)
    for e in range(n_local):
        ready(f'eg{e}', f'eu{e}')
        act(1, same, e)
    recv('gd1', 'gd2', 'd1')
    set_gates(1, 1)
    for e in range(n_local):
        act(1, other, e)
    for e in range(n_local):
        ready(f'ed{e}')
    down(1)
    recv('f1a', 'f2a', 'f1b', 'f2b')
    send('d3')
    recv('g3')
    send('gd3')
    set_gates(3, 0)
    act(3, same, 0)
    send_near()
    for e in range(1, n_local):
        act(3, same, e)
    recv('gd3', 'd3')
    set_gates(3, 1)
    for e in range(n_local):
        act(3, other, e)
    recv('a3a', 'a3b', 'a4a', 'a4b')
    send('d2')
    down(3)
    set_gates(2, 0)
    for e in range(n_local):
        act(2, same, e)
    send_far()
    recv('d2')
    set_gates(2, 1)
    for e in range(n_local):
        act(2, other, e)
    down(2)
    recv('d0', 'gd0')
    set_gates(0, 0)
    set_gates(0, 1)
    act(0, both, 0)
    act(0, both, 1)
    for n in range(N_P):
        add_partner(2, n)
    act(0, both, 2)
    act(0, both, 3)
    pass_on(0)
    down(0)
    pass_on(1)

    normed_ffn = rms_rows(att[...], norm_row(v_fn))
    n_ffn = ff_dim // FF_BLOCK
    for b in range(n_ffn):
        if (b * FF_BLOCK) % 1024 == 0:
            i = b * FF_BLOCK // 1024
            ready(f'fg{i}', f'fu{i}', f'fd{i}')
        ffn_block(b, normed_ffn)
        if b == 2:
            pass_on(2)
        if b == 5:
            pass_on(3)
    for n in range(N_P):
        add_partner(0, n)
    ffn_acc[...] = ffn_acc[...] + p_buf[0, :tokens]
    for n in range(N_P):
        recv(f'i1_{n}', f'i2_{n}')
    ffn_acc[:half] = ffn_acc[:half] + rb[0, :half]
    ffn_acc[half:] = ffn_acc[half:] + rb[1, half:]
    stores = []
    for n in range(N_O):
        recv(f'w1_{n}', f'w2_{n}')
        cols = slice(n * model // N_O, (n + 1) * model // N_O)
        v_out[:half, cols] = (ffn_acc[:half, cols] + rb[1, :half, cols]).astype(BF16)
        v_out[half:, cols] = (ffn_acc[half:, cols] + rb[0, half:, cols]).astype(BF16)
        stores.append(pltpu.make_async_copy(v_out.at[:, o_cols[n]], out.at[:, o_cols[n]], w_sem.at[len(loads) + n]))
        stores[-1].start()
    for copy in copies.values():
        copy.wait_send()
    for copy in stores:
        copy.wait()


def solution(mesh):
    group = mesh.shape['ep']
    row_spec = P(('dp', 'ep'), None, None)
    vec_spec = P(None)
    mat_spec = P(None, None)
    cube_spec = P(None, None, None)
    expert_spec = P('ep', None, None)

    def per_device(hidden, expert_ids, slot_ids, attn_norm, w_query, w_key, w_value, w_out, ffn_norm, ffn_gate, ffn_up, ffn_down, moe_norm, w_router, exp_gate, exp_up, exp_down):
        n_seqs, seq_len, model = hidden.shape
        tokens = n_seqs * seq_len
        n_heads, head_dim = w_out.shape[0], w_out.shape[1]
        top_k = expert_ids.shape[-1]
        n_local, _, exp_ff = exp_gate.shape
        n_experts = w_router.shape[1]
        kv_dim = w_key.shape[1]
        assert n_seqs == 1 and group == 8 and head_dim == 64
        cos_t, sin_t = rope_tables(seq_len, head_dim)
        args = (hidden.reshape(tokens, model), expert_ids.reshape(tokens, top_k).T, attn_norm.reshape(-1, LANES),
                w_query, w_key, w_value, w_out.reshape(n_heads * head_dim, model), ffn_norm.reshape(-1, LANES),
                ffn_gate, ffn_up, ffn_down, moe_norm.reshape(-1, LANES), w_router.T, exp_gate, exp_up, exp_down,
                jnp.asarray(cos_t), jnp.asarray(sin_t))
        vmem = [pltpu.VMEM(a.shape, a.dtype) for a in args]
        scratch = vmem + [
            pltpu.VMEM((tokens, model), BF16),
            pltpu.VMEM((4, 2 * tokens, model), BF16),
            pltpu.VMEM((4, 2, n_experts, tokens), F32),
            pltpu.VMEM((4, 2 * tokens, model), F32),
            pltpu.VMEM((4, tokens, model), F32),
            pltpu.VMEM((tokens, model), F32),
            pltpu.VMEM((2, tokens, model), F32),
            pltpu.VMEM((tokens, n_heads * head_dim), F32),
            pltpu.VMEM((tokens, kv_dim), F32),
            pltpu.VMEM((tokens, kv_dim), F32),
            pltpu.VMEM((tokens, n_heads * head_dim), BF16),
            pltpu.VMEM((2 * tokens, n_local * exp_ff), BF16),
            pltpu.VMEM((n_local, 2 * tokens, LANES), F32),
            pltpu.VMEM((tokens, model), BF16),
            pltpu.VMEM((tokens, model), F32),
            pltpu.SemaphoreType.DMA((48,)),
            pltpu.SemaphoreType.DMA((56,)),
            pltpu.SemaphoreType.DMA((56,)),
        ]
        result = pl.pallas_call(
            functools.partial(kernel, group),
            out_shape=jax.ShapeDtypeStruct((tokens, model), BF16),
            in_specs=[pl.BlockSpec(memory_space=pl.ANY)] * len(args),
            out_specs=pl.BlockSpec(memory_space=pl.ANY),
            scratch_shapes=scratch,
            compiler_params=pltpu.CompilerParams(collective_id=0, has_side_effects=True, vmem_limit_bytes=67043328),
        )(*args)
        return result.reshape(n_seqs, seq_len, model)

    return jax.shard_map(per_device, mesh=mesh, in_specs=(row_spec, row_spec, row_spec, vec_spec, mat_spec, mat_spec, mat_spec, cube_spec, vec_spec, mat_spec, mat_spec, mat_spec, vec_spec, mat_spec, expert_spec, expert_spec, expert_spec), out_specs=row_spec, check_vma=False)
```

time: 51.3 us -> 40.5 us (0.79)
  local copies, waits for them, and re-layouts: 8.57 us -> 1.67 us
  Pallas kernels: 42.5 us -> 38.8 us
    reshape x3 -> x0, local copies, waits for them, and re-layouts: 3.82 us -> none  [the longest x1 1.28 us: per_device(): attn_norm.reshape(1, model)]
    pallas_call x1, Pallas kernels: 42.5 us -> 38.8 us  [per_device(): pl.pallas_call(functools.partial(kernel, group), out_shape=jax.ShapeDtype...]
    unnamed x3 -> x1, local copies, waits for them, and re-layouts: 4.75 us -> 1.67 us
where the time goes in v2:
time: 40.5 us; the launch traced here: 40.4 us
  Pallas kernels  38.8 us (96%)
  local copies, waits for them, and re-layouts  1.67 us (4%)
    pallas_call x1, Pallas kernels, per_device(): pl.pallas_call(functools.partial(kernel, group), out_shape=jax.ShapeDtype...  38.8 us
    unnamed x1, local copies, waits for them, and re-layouts  1.67 us

profile of v2, /device:TPU:112, one launch (start us, length us, event | category | flops | bytes accessed | tf_op | source)
XLA Modules:
  0.0 40.4 jit_solution(447404333583779456)
XLA Ops:
  0.0 38.8 %shard_map.172 = bf16[128,1024]{1,0:T(8,128)(2,1)} custom-call(bf16[128,1024]{1,0:T(8,128)(2,1)} %bitcast.12, s32[8,128]{1,0:T(8,128)} %bitcast.14, bf16[8,128]{1,0:T(8,128)(2,1)} %bitcast.15, bf16[1024,1024]{1,0:T(8,128)(2,1)} %w_query.1, bf16[1024,512]{1,0:T(8,128)(2,1)} %w_key.1, bf16[1024,512]{1,0:T(8,128)(2,1)} %w_value.1, bf16[1024,1024]{1,0:T(8,128)(2,1)} %bitcast.10, ...), custom_call_target="tpu_custom_call" | custom-call | tf_op jit(solution)/shard_map/pallas_call | solution.py:410
  38.8 1.7 %copy.20 = bf16[1,128,1024]{2,1,0:T(8,128)(2,1)} copy(bf16[1,128,1024]{2,1,0:T(8,128)(2,1)} %bitcast.11) | data formatting | bytes 524288

commit v3 on v2

--- a/solution.py
+++ b/solution.py
@@ -15,8 +15,8 @@
 LANES = 128
 FF_BLOCK = 512
 COL = 256
-N_P = 2
-N_O = 4
+N_P = 4
+VMEM_BYTES = 60 * 1024 * 1024
 
 
 def rms_rows(row_vals, norm_scale):
@@ -43,9 +43,9 @@
 
 
 def kernel(group, hidden, ids, attn_norm, w_query, w_key, w_value, w_out, ffn_norm, ffn_gate, ffn_up, ffn_down,
-           moe_norm, w_router, exp_gate, exp_up, exp_down, cos_t, sin_t, out,
+           moe_norm, w_router, exp_gate, exp_up, exp_down, cos_t, sin_t, total, far,
            v_hid, v_ids, v_an, v_wq, v_wk, v_wv, v_wo, v_fn, v_fg, v_fu, v_fd, v_mn, v_wr, v_eg, v_eu, v_ed, v_cos, v_sin,
-           v_out, x_buf, g_buf, p_buf, pr_buf, tb, rb, qf, kf, vf, ctx, hb, gate_b, att, ffn_acc,
+           x_buf, g_buf, p_buf, pr_buf, tb, near, qf, kf, vf, ctx, hb, gate_b, att, ffn_acc,
            w_sem, s_sem, r_sem):
     tokens, model = v_hid.shape
     half, quarter = tokens // 2, tokens // 4
@@ -87,7 +87,6 @@
     lo, hi, al, ot = pl.ds(0, half), pl.ds(half, half), pl.ds(0, tokens), pl.ds(tokens, tokens)
     q0, q1, q2, q3 = (pl.ds(i * quarter, quarter) for i in range(4))
     p_cols = [pl.ds(n * model // N_P, model // N_P) for n in range(N_P)]
-    o_cols = [pl.ds(n * model // N_O, model // N_O) for n in range(N_O)]
     for name, c_src, rows, c_dst, device in (
             ('a1a', 0, q0, 1, right), ('a1b', 0, q1, 1, right), ('a2a', 0, q2, 1, left), ('a2b', 0, q3, 1, left),
             ('a3a', 0, q2, 2, right), ('a3b', 0, q3, 2, right), ('a4a', 0, q0, 2, left), ('a4b', 0, q1, 2, left),
@@ -103,13 +102,12 @@
     for n, cols in enumerate(p_cols):
         for c in range(4):
             remote(f'p{c}_{n}', p_buf.at[c, ot, cols], pr_buf.at[c, :, cols], partner)
-        remote(f'i1_{n}', p_buf.at[1, hi, cols], rb.at[1, hi, cols], right)
-        remote(f'i2_{n}', p_buf.at[1, lo, cols], rb.at[0, lo, cols], left)
-    for n, cols in enumerate(o_cols):
+        remote(f'i1_{n}', p_buf.at[1, hi, cols], near.at[hi, cols], right)
+        remote(f'i2_{n}', p_buf.at[1, lo, cols], near.at[lo, cols], left)
         remote(f'o1_{n}', p_buf.at[3, lo, cols], tb.at[lo, cols], right)
         remote(f'o2_{n}', p_buf.at[3, hi, cols], tb.at[hi, cols], left)
-        remote(f'w1_{n}', p_buf.at[2, lo, cols], rb.at[1, lo, cols], right)
-        remote(f'w2_{n}', p_buf.at[2, hi, cols], rb.at[0, hi, cols], left)
+        remote(f'w1_{n}', p_buf.at[2, lo, cols], far.at[lo, cols], right)
+        remote(f'w2_{n}', p_buf.at[2, hi, cols], far.at[hi, cols], left)
 
     load('hid', hidden, v_hid)
     load('mn', moe_norm, v_mn)
@@ -119,6 +117,7 @@
     load('wq', w_query, v_wq)
     load('wk', w_key, v_wk)
     load('wv', w_value, v_wv)
+    load('fn', ffn_norm, v_fn)
     load('cos', cos_t, v_cos)
     load('sin', sin_t, v_sin)
 
@@ -132,7 +131,6 @@
         load(f'eu{e}', exp_up.at[e], v_eu.at[e])
     for e in range(n_local):
         load(f'ed{e}', exp_down.at[e], v_ed.at[e])
-    load('fn', ffn_norm, v_fn)
 
     def norm_row(ref):
         scale = ref[...].astype(F32)
@@ -229,19 +227,17 @@
         cols = slice(n * model // N_P, (n + 1) * model // N_P)
         p_buf[c, :tokens, cols] = p_buf[c, :tokens, cols] + pr_buf[c, :, cols]
 
-    def send_near():
-        for n in range(N_P):
-            add_partner(1, n)
-            send(f'i1_{n}', f'i2_{n}')
-
-    def send_far():
-        for n in range(N_P):
-            add_partner(3, n)
-            for k in range(n * N_O // N_P, (n + 1) * N_O // N_P):
-                send(f'o1_{k}', f'o2_{k}')
+    def send_near(n):
+        add_partner(1, n)
+        send(f'i1_{n}', f'i2_{n}')
+
+    def send_far(n):
+        add_partner(3, n)
+        send(f'o1_{n}', f'o2_{n}')
 
     def pass_on(n):
-        cols = slice(n * model // N_O, (n + 1) * model // N_O)
+        add_partner(2, n)
+        cols = slice(n * model // N_P, (n + 1) * model // N_P)
         recv(f'o1_{n}')
         p_buf[2, :half, cols] = p_buf[2, :half, cols] + tb[:half, cols]
         send(f'w1_{n}')
@@ -272,9 +268,9 @@
     ready('wo', 'fn')
     att[...] = (v_hid[...].astype(F32) + dot(ctx[...], v_wo[...])).astype(BF16)
     recv('a1b', 'a2b')
-    send('f1b', 'f2b', 'd1', 'a3b', 'a4b')
+    send('f1b', 'f2b', 'd1')
     recv('g1', 'g2')
-    send('g3', 'gd1', 'gd2')
+    send('g3', 'gd1', 'gd2', 'a3b', 'a4b')
 
     n_blk = ff_dim // 1024
     for b in range(n_blk):
@@ -294,13 +290,16 @@
     for e in range(n_local):
         ready(f'ed{e}')
     down(1)
+    send_near(0)
     recv('f1a', 'f2a', 'f1b', 'f2b')
     send('d3')
     recv('g3')
     send('gd3')
+    send_near(1)
     set_gates(3, 0)
     act(3, same, 0)
-    send_near()
+    send_near(2)
+    send_near(3)
     for e in range(1, n_local):
         act(3, same, e)
     recv('gd3', 'd3')
@@ -311,9 +310,14 @@
     send('d2')
     down(3)
     set_gates(2, 0)
-    for e in range(n_local):
-        act(2, same, e)
-    send_far()
+    act(2, same, 0)
+    send_far(0)
+    act(2, same, 1)
+    send_far(1)
+    act(2, same, 2)
+    send_far(2)
+    act(2, same, 3)
+    send_far(3)
     recv('d2')
     set_gates(2, 1)
     for e in range(n_local):
@@ -322,12 +326,8 @@
     recv('d0', 'gd0')
     set_gates(0, 0)
     set_gates(0, 1)
-    act(0, both, 0)
-    act(0, both, 1)
-    for n in range(N_P):
-        add_partner(2, n)
-    act(0, both, 2)
-    act(0, both, 3)
+    for e in range(n_local):
+        act(0, both, e)
     pass_on(0)
     down(0)
     pass_on(1)
@@ -339,29 +339,21 @@
             i = b * FF_BLOCK // 1024
             ready(f'fg{i}', f'fu{i}', f'fd{i}')
         ffn_block(b, normed_ffn)
-        if b == 2:
-            pass_on(2)
-        if b == 5:
-            pass_on(3)
+        if b in (1, 3):
+            pass_on((b + 3) // 2)
     for n in range(N_P):
         add_partner(0, n)
     ffn_acc[...] = ffn_acc[...] + p_buf[0, :tokens]
     for n in range(N_P):
         recv(f'i1_{n}', f'i2_{n}')
-    ffn_acc[:half] = ffn_acc[:half] + rb[0, :half]
-    ffn_acc[half:] = ffn_acc[half:] + rb[1, half:]
-    stores = []
-    for n in range(N_O):
-        recv(f'w1_{n}', f'w2_{n}')
-        cols = slice(n * model // N_O, (n + 1) * model // N_O)
-        v_out[:half, cols] = (ffn_acc[:half, cols] + rb[1, :half, cols]).astype(BF16)
-        v_out[half:, cols] = (ffn_acc[half:, cols] + rb[0, half:, cols]).astype(BF16)
-        stores.append(pltpu.make_async_copy(v_out.at[:, o_cols[n]], out.at[:, o_cols[n]], w_sem.at[len(loads) + n]))
-        stores[-1].start()
-    for copy in copies.values():
-        copy.wait_send()
-    for copy in stores:
-        copy.wait()
+    late = tuple(f'w{k}_{n}' for k in (1, 2) for n in range(N_P))
+    for name, copy in copies.items():
+        if name not in late:
+            copy.wait_send()
+    total[...] = ffn_acc[...] + near[...]
+    for name in late:
+        copies[name].wait_recv()
+        copies[name].wait_send()
 
 
 def solution(mesh):
@@ -388,13 +380,12 @@
                 jnp.asarray(cos_t), jnp.asarray(sin_t))
         vmem = [pltpu.VMEM(a.shape, a.dtype) for a in args]
         scratch = vmem + [
-            pltpu.VMEM((tokens, model), BF16),
             pltpu.VMEM((4, 2 * tokens, model), BF16),
             pltpu.VMEM((4, 2, n_experts, tokens), F32),
             pltpu.VMEM((4, 2 * tokens, model), F32),
             pltpu.VMEM((4, tokens, model), F32),
             pltpu.VMEM((tokens, model), F32),
-            pltpu.VMEM((2, tokens, model), F32),
+            pltpu.VMEM((tokens, model), F32),
             pltpu.VMEM((tokens, n_heads * head_dim), F32),
             pltpu.VMEM((tokens, kv_dim), F32),
             pltpu.VMEM((tokens, kv_dim), F32),
@@ -404,17 +395,17 @@
             pltpu.VMEM((tokens, model), BF16),
             pltpu.VMEM((tokens, model), F32),
             pltpu.SemaphoreType.DMA((48,)),
-            pltpu.SemaphoreType.DMA((56,)),
-            pltpu.SemaphoreType.DMA((56,)),
+            pltpu.SemaphoreType.DMA((64,)),
+            pltpu.SemaphoreType.DMA((64,)),
         ]
-        result = pl.pallas_call(
+        total, far = pl.pallas_call(
             functools.partial(kernel, group),
-            out_shape=jax.ShapeDtypeStruct((tokens, model), BF16),
+            out_shape=(pltpu.VMEM((tokens, model), F32), pltpu.VMEM((tokens, model), F32)),
             in_specs=[pl.BlockSpec(memory_space=pl.ANY)] * len(args),
-            out_specs=pl.BlockSpec(memory_space=pl.ANY),
+            out_specs=(pl.BlockSpec(memory_space=pltpu.VMEM),) * 2,
             scratch_shapes=scratch,
-            compiler_params=pltpu.CompilerParams(collective_id=0, has_side_effects=True, vmem_limit_bytes=67043328),
+            compiler_params=pltpu.CompilerParams(collective_id=0, has_side_effects=True, vmem_limit_bytes=VMEM_BYTES),
         )(*args)
-        return result.reshape(n_seqs, seq_len, model)
+        return (total + far).astype(BF16).reshape(n_seqs, seq_len, model)
 
     return jax.shard_map(per_device, mesh=mesh, in_specs=(row_spec, row_spec, row_spec, vec_spec, mat_spec, mat_spec, mat_spec, cube_spec, vec_spec, mat_spec, mat_spec, mat_spec, vec_spec, mat_spec, expert_spec, expert_spec, expert_spec), out_specs=row_spec, check_vma=False)

time: 40.5 us -> 40 us (0.988)
  local copies, waits for them, and re-layouts: 1.67 us -> 0 us
  other arithmetic: 0 us -> 0.77 us
    unnamed x1 -> x0, local copies, waits for them, and re-layouts: 1.67 us -> none
    reshape x0 -> x1, other arithmetic: none -> 0.77 us  [per_device(): return (total + far).astype(BF16).reshape(n_seqs, seq_len, model)]
where the time goes in v3:
time: 40 us; the launch traced here: 39.7 us
  Pallas kernels  38.9 us (97%)
  other arithmetic  0.77 us (2%)
    pallas_call x1, Pallas kernels, per_device(): pl.pallas_call(functools.partial(kernel, group), out_shape=(pltpu.VMEM((t...  38.9 us

profile of v3, /device:TPU:112, one launch (start us, length us, event | category | flops | bytes accessed | tf_op | source)
XLA Modules:
  0.0 39.7 jit_solution(349796292813714696)
XLA Ops:
  0.0 38.9 %shard_map.172 = (f32[128,1024]{1,0:T(8,128)S(1)}, f32[128,1024]{1,0:T(8,128)S(1)}) custom-call(bf16[128,1024]{1,0:T(8,128)(2,1)} %bitcast.12, s32[8,128]{1,0:T(8,128)} %bitcast.14, bf16[8,128]{1,0:T(8,128)(2,1)} %bitcast.15, bf16[1024,1024]{1,0:T(8,128)(2,1)} %w_query.1, bf16[1024,512]{1,0:T(8,128)(2,1)} %w_key.1, bf16[1024,512]{1,0:T(8,128)(2,1)} %w_value.1, ...), custom_call_target="tpu_custom_call" | custom-call | tf_op jit(solution)/shard_map/pallas_call | solution.py:401
  38.9 0.8 %fusion = bf16[1,128,1024]{2,1,0:T(8,128)(2,1)} fusion(f32[128,1024]{1,0:T(8,128)S(1)} %get-tuple-element.7, f32[128,1024]{1,0:T(8,128)S(1)} %get-tuple-element.8), kind=kLoop, calls=%fused_computation.1 | loop fusion | flops 262144 | bytes 1310720 | tf_op jit(solution)/shard_map/reshape | solution.py:409

commit v4 on v3

--- a/solution.py
+++ b/solution.py
@@ -15,7 +15,8 @@
 LANES = 128
 FF_BLOCK = 512
 COL = 256
-N_P = 4
+N_P = 2
+N_O = 4
 VMEM_BYTES = 60 * 1024 * 1024
 
 
@@ -104,6 +105,8 @@
             remote(f'p{c}_{n}', p_buf.at[c, ot, cols], pr_buf.at[c, :, cols], partner)
         remote(f'i1_{n}', p_buf.at[1, hi, cols], near.at[hi, cols], right)
         remote(f'i2_{n}', p_buf.at[1, lo, cols], near.at[lo, cols], left)
+    o_cols = [pl.ds(n * model // N_O, model // N_O) for n in range(N_O)]
+    for n, cols in enumerate(o_cols):
         remote(f'o1_{n}', p_buf.at[3, lo, cols], tb.at[lo, cols], right)
         remote(f'o2_{n}', p_buf.at[3, hi, cols], tb.at[hi, cols], left)
         remote(f'w1_{n}', p_buf.at[2, lo, cols], far.at[lo, cols], right)
@@ -201,26 +204,24 @@
         gates_c = gt.T
         for e in range(n_local):
             gate = jnp.sum(jnp.where(e_lane == e, gates_c, 0.0), axis=-1, keepdims=True)
-            gate_b[e, par * tokens:(par + 1) * tokens] = jnp.broadcast_to(gate, (tokens, LANES))
+            gate_b[int(c == 0), e, par * tokens:(par + 1) * tokens] = jnp.broadcast_to(gate, (tokens, LANES))
 
     def act(c, rows, e):
         x = x_buf[c, rows]
-        used = gate_b[e, rows] > 0.0
-        used = jnp.concatenate([used.astype(F32)] * (COL // LANES), axis=1) > 0.0
+        used = jnp.concatenate([gate_b[int(c == 0), e, rows]] * (COL // LANES), axis=1) > 0.0
         for n in range(exp_ff // COL):
             cols = slice(n * COL, (n + 1) * COL)
             z = silu(dot(x, v_eg[e, :, cols])) * dot(x, v_eu[e, :, cols])
-            hb[rows, e * exp_ff + n * COL:e * exp_ff + (n + 1) * COL] = jnp.where(used, z, 0.0).astype(BF16)
-
-    def down(c):
-        for n in range(model // COL):
+            hb[int(c == 0), rows, e * exp_ff + n * COL:e * exp_ff + (n + 1) * COL] = jnp.where(used, z, 0.0).astype(BF16)
+
+    def down(c, part):
+        for n in range(part * model // N_P // COL, (part + 1) * model // N_P // COL):
             cols = slice(n * COL, (n + 1) * COL)
             for e in range(n_local):
-                y = dot(hb[:, e * exp_ff:(e + 1) * exp_ff], v_ed[e, :, cols]).astype(BF16).astype(F32)
-                y = y * jnp.concatenate([gate_b[e]] * (COL // LANES), axis=1)
+                y = dot(hb[int(c == 0), :, e * exp_ff:(e + 1) * exp_ff], v_ed[e, :, cols]).astype(BF16).astype(F32)
+                y = y * jnp.concatenate([gate_b[int(c == 0), e]] * (COL // LANES), axis=1)
                 p_buf[c, :, cols] = y if e == 0 else p_buf[c, :, cols] + y
-            if (n + 1) * COL % (model // N_P) == 0:
-                send(f'p{c}_{((n + 1) * COL) // (model // N_P) - 1}')
+        send(f'p{c}_{part}')
 
     def add_partner(c, n):
         recv(f'p{c}_{n}')
@@ -233,32 +234,27 @@
 
     def send_far(n):
         add_partner(3, n)
-        send(f'o1_{n}', f'o2_{n}')
+        send(*(f'o{k}_{m}' for m in range(n * N_O // N_P, (n + 1) * N_O // N_P) for k in (1, 2)))
 
     def pass_on(n):
-        add_partner(2, n)
-        cols = slice(n * model // N_P, (n + 1) * model // N_P)
-        recv(f'o1_{n}')
-        p_buf[2, :half, cols] = p_buf[2, :half, cols] + tb[:half, cols]
-        send(f'w1_{n}')
-        recv(f'o2_{n}')
-        p_buf[2, half:tokens, cols] = p_buf[2, half:tokens, cols] + tb[half:, cols]
-        send(f'w2_{n}')
+        cols = slice(n * model // N_O, (n + 1) * model // N_O)
+        recv(f'o1_{n}', f'o2_{n}')
+        p_buf[2, :tokens, cols] = p_buf[2, :tokens, cols] + tb[:, cols]
+        send(f'w1_{n}', f'w2_{n}')
 
     def ffn_block(b, x):
         act_cols = slice(b * FF_BLOCK, (b + 1) * FF_BLOCK)
         for n in range(FF_BLOCK // COL):
             cols = slice(b * FF_BLOCK + n * COL, b * FF_BLOCK + (n + 1) * COL)
             z = silu(dot(x, v_fg[:, cols])) * dot(x, v_fu[:, cols])
-            hb[:tokens, n * COL:(n + 1) * COL] = z.astype(BF16)
-        h = hb[:tokens, :FF_BLOCK]
+            hb[0, :tokens, n * COL:(n + 1) * COL] = z.astype(BF16)
+        h = hb[0, :tokens, :FF_BLOCK]
         for n in range(model // COL):
             cols = slice(n * COL, (n + 1) * COL)
             y = dot(h, v_fd[act_cols, cols])
             ffn_acc[:, cols] = y + (att[:, cols].astype(F32) if b == 0 else ffn_acc[:, cols])
 
     same, other, both = slice(0, tokens), slice(tokens, 2 * tokens), slice(0, 2 * tokens)
-
     attend(0)
     attend(1)
     attend(2)
@@ -279,78 +275,74 @@
         load(f'fu{b}', ffn_up.at[:, cols], v_fu.at[:, cols])
         load(f'fd{b}', ffn_down.at[cols], v_fd.at[cols])
 
+    for e in range(n_local):
+        ready(f'eg{e}', f'eu{e}')
     set_gates(1, 0)
     for e in range(n_local):
-        ready(f'eg{e}', f'eu{e}')
         act(1, same, e)
     recv('gd1', 'gd2', 'd1')
+    for e in range(n_local):
+        ready(f'ed{e}')
     set_gates(1, 1)
     for e in range(n_local):
         act(1, other, e)
-    for e in range(n_local):
-        ready(f'ed{e}')
-    down(1)
-    send_near(0)
+    down(1, 0)
+    down(1, 1)
     recv('f1a', 'f2a', 'f1b', 'f2b')
     send('d3')
     recv('g3')
     send('gd3')
-    send_near(1)
-    set_gates(3, 0)
-    act(3, same, 0)
-    send_near(2)
-    send_near(3)
-    for e in range(1, n_local):
-        act(3, same, e)
-    recv('gd3', 'd3')
-    set_gates(3, 1)
-    for e in range(n_local):
-        act(3, other, e)
-    recv('a3a', 'a3b', 'a4a', 'a4b')
-    send('d2')
-    down(3)
-    set_gates(2, 0)
-    act(2, same, 0)
-    send_far(0)
-    act(2, same, 1)
-    send_far(1)
-    act(2, same, 2)
-    send_far(2)
-    act(2, same, 3)
-    send_far(3)
-    recv('d2')
-    set_gates(2, 1)
-    for e in range(n_local):
-        act(2, other, e)
-    down(2)
     recv('d0', 'gd0')
     set_gates(0, 0)
     set_gates(0, 1)
-    for e in range(n_local):
-        act(0, both, e)
+    act(0, both, 0)
+    send_near(0)
+    act(0, both, 1)
+    send_near(1)
+    recv('gd3', 'd3')
+    set_gates(3, 0)
+    set_gates(3, 1)
+    for e in range(n_local):
+        act(3, both, e)
+    recv('a3a', 'a3b', 'a4a', 'a4b')
+    send('d2')
+    down(3, 0)
+    down(3, 1)
+    act(0, both, 2)
+    send_far(0)
+    act(0, both, 3)
+    send_far(1)
+    recv('d2')
+    set_gates(2, 0)
+    set_gates(2, 1)
+    for e in range(n_local):
+        act(2, both, e)
+    down(2, 0)
+    down(2, 1)
+    down(0, 0)
+    add_partner(2, 0)
     pass_on(0)
-    down(0)
+    down(0, 1)
+    add_partner(2, 1)
     pass_on(1)
-
+    for b in range(n_blk):
+        ready(f'fg{b}', f'fu{b}', f'fd{b}')
     normed_ffn = rms_rows(att[...], norm_row(v_fn))
     n_ffn = ff_dim // FF_BLOCK
     for b in range(n_ffn):
-        if (b * FF_BLOCK) % 1024 == 0:
-            i = b * FF_BLOCK // 1024
-            ready(f'fg{i}', f'fu{i}', f'fd{i}')
         ffn_block(b, normed_ffn)
-        if b in (1, 3):
-            pass_on((b + 3) // 2)
+        if b == 0:
+            pass_on(2)
+        if b == 2:
+            pass_on(3)
     for n in range(N_P):
         add_partner(0, n)
-    ffn_acc[...] = ffn_acc[...] + p_buf[0, :tokens]
-    for n in range(N_P):
         recv(f'i1_{n}', f'i2_{n}')
-    late = tuple(f'w{k}_{n}' for k in (1, 2) for n in range(N_P))
+    late = tuple(f'w{k}_{n}' for k in (1, 2) for n in range(N_O))
     for name, copy in copies.items():
         if name not in late:
             copy.wait_send()
-    total[...] = ffn_acc[...] + near[...]
+    total[...] = ffn_acc[...] + p_buf[0, :tokens] + near[...]
     for name in late:
         copies[name].wait_recv()
         copies[name].wait_send()
@@ -390,8 +382,8 @@
             pltpu.VMEM((tokens, kv_dim), F32),
             pltpu.VMEM((tokens, kv_dim), F32),
             pltpu.VMEM((tokens, n_heads * head_dim), BF16),
-            pltpu.VMEM((2 * tokens, n_local * exp_ff), BF16),
-            pltpu.VMEM((n_local, 2 * tokens, LANES), F32),
+            pltpu.VMEM((2, 2 * tokens, n_local * exp_ff), BF16),
+            pltpu.VMEM((2, n_local, 2 * tokens, LANES), F32),
             pltpu.VMEM((tokens, model), BF16),
             pltpu.VMEM((tokens, model), F32),
             pltpu.SemaphoreType.DMA((48,)),

time: 40 us -> 36.9 us (0.922)
  Pallas kernels: 38.9 us -> 36.1 us
    pallas_call x1, Pallas kernels: 38.9 us -> 36.1 us  [per_device(): pl.pallas_call(functools.partial(kernel, group), out_shape=(pltpu.VMEM((t...]
where the time goes in v4:
time: 36.9 us; the launch traced here: 36.8 us
  Pallas kernels  36.1 us (98%)
  other arithmetic  0.77 us (2%)
    pallas_call x1, Pallas kernels, per_device(): pl.pallas_call(functools.partial(kernel, group), out_shape=(pltpu.VMEM((t...  36.1 us
    reshape x1, other arithmetic, per_device(): return (total + far).astype(BF16).reshape(n_seqs, seq_len, model)  0.77 us

profile of v4, /device:TPU:112, one launch (start us, length us, event | category | flops | bytes accessed | tf_op | source)
XLA Modules:
  0.0 36.8 jit_solution(17002129409167317620)
XLA Ops:
  0.0 36.1 %shard_map.172 = (f32[128,1024]{1,0:T(8,128)S(1)}, f32[128,1024]{1,0:T(8,128)S(1)}) custom-call(bf16[128,1024]{1,0:T(8,128)(2,1)} %bitcast.12, s32[8,128]{1,0:T(8,128)} %bitcast.14, bf16[8,128]{1,0:T(8,128)(2,1)} %bitcast.15, bf16[1024,1024]{1,0:T(8,128)(2,1)} %w_query.1, bf16[1024,512]{1,0:T(8,128)(2,1)} %w_key.1, bf16[1024,512]{1,0:T(8,128)(2,1)} %w_value.1, ...), custom_call_target="tpu_custom_call" | custom-call | tf_op jit(solution)/shard_map/pallas_call | solution.py:393
  36.1 0.8 %fusion = bf16[1,128,1024]{2,1,0:T(8,128)(2,1)} fusion(f32[128,1024]{1,0:T(8,128)S(1)} %get-tuple-element.7, f32[128,1024]{1,0:T(8,128)S(1)} %get-tuple-element.8), kind=kLoop, calls=%fused_computation.1 | loop fusion | flops 262144 | bytes 1310720 | tf_op jit(solution)/shard_map/reshape | solution.py:401

commit v5 on v4

--- a/solution.py
+++ b/solution.py
@@ -16,7 +16,6 @@
 FF_BLOCK = 512
 COL = 256
 N_P = 2
-N_O = 4
 VMEM_BYTES = 60 * 1024 * 1024
 
 
@@ -27,7 +26,8 @@
 
 
 def silu(z):
-    return z / (1.0 + jnp.exp(-z))
+    half = 0.5 * z
+    return half + half * jnp.tanh(half)
 
 
 def dot(a, b):
@@ -85,32 +85,39 @@
         for name in names:
             copies[name].wait_recv()
 
-    lo, hi, al, ot = pl.ds(0, half), pl.ds(half, half), pl.ds(0, tokens), pl.ds(tokens, tokens)
-    q0, q1, q2, q3 = (pl.ds(i * quarter, quarter) for i in range(4))
+    al, ot = pl.ds(0, tokens), pl.ds(tokens, tokens)
+
+    def place(c, par, q):
+        if c in (0, 2):
+            return pl.ds(par * tokens + q * quarter, quarter)
+        return pl.ds((q % 2) * tokens + par * half + (q // 2) * quarter, quarter)
+
+    for name, c_src, q, c_dst, device in (
+            ('a1a', 0, 0, 1, right), ('a1b', 0, 1, 1, right), ('a2a', 0, 2, 1, left), ('a2b', 0, 3, 1, left),
+            ('a3a', 0, 2, 2, right), ('a3b', 0, 3, 2, right), ('a4a', 0, 0, 2, left), ('a4b', 0, 1, 2, left),
+            ('f1a', 1, 0, 3, right), ('f1b', 1, 1, 3, right), ('f2a', 1, 2, 3, left), ('f2b', 1, 3, 3, left)):
+        remote(name, x_buf.at[c_src, place(c_src, 0, q)], x_buf.at[c_dst, place(c_dst, 0, q)], device)
     p_cols = [pl.ds(n * model // N_P, model // N_P) for n in range(N_P)]
-    for name, c_src, rows, c_dst, device in (
-            ('a1a', 0, q0, 1, right), ('a1b', 0, q1, 1, right), ('a2a', 0, q2, 1, left), ('a2b', 0, q3, 1, left),
-            ('a3a', 0, q2, 2, right), ('a3b', 0, q3, 2, right), ('a4a', 0, q0, 2, left), ('a4b', 0, q1, 2, left),
-            ('f1a', 1, q0, 3, right), ('f1b', 1, q1, 3, right), ('f2a', 1, q2, 3, left), ('f2b', 1, q3, 3, left)):
-        remote(name, x_buf.at[c_src, rows], x_buf.at[c_dst, rows], device)
-    for c in range(4):
+    for c in (0, 2):
         remote(f'd{c}', x_buf.at[c, al], x_buf.at[c, ot], partner)
+        for n, cols in enumerate(p_cols):
+            remote(f'p{c}_{n}', p_buf.at[c, ot, cols], pr_buf.at[c, :, cols], partner)
+    for c in (1, 3):
+        for n, part in enumerate('ab'):
+            remote(f'd{c}{part}', x_buf.at[c, pl.ds(n * tokens, half)], x_buf.at[c, pl.ds(n * tokens + half, half)], partner)
+            remote(f'p{c}{part}', p_buf.at[c, pl.ds(n * tokens + half, half)], pr_buf.at[c, pl.ds(n * half, half)], partner)
     remote('g1', g_buf.at[0, 0], g_buf.at[1, 0], right)
     remote('g2', g_buf.at[0, 0], g_buf.at[2, 0], left)
     remote('g3', g_buf.at[1, 0], g_buf.at[3, 0], right)
     for c in range(4):
         remote(f'gd{c}', g_buf.at[c, 0], g_buf.at[c, 1], partner)
-    for n, cols in enumerate(p_cols):
-        for c in range(4):
-            remote(f'p{c}_{n}', p_buf.at[c, ot, cols], pr_buf.at[c, :, cols], partner)
-        remote(f'i1_{n}', p_buf.at[1, hi, cols], near.at[hi, cols], right)
-        remote(f'i2_{n}', p_buf.at[1, lo, cols], near.at[lo, cols], left)
-    o_cols = [pl.ds(n * model // N_O, model // N_O) for n in range(N_O)]
-    for n, cols in enumerate(o_cols):
-        remote(f'o1_{n}', p_buf.at[3, lo, cols], tb.at[lo, cols], right)
-        remote(f'o2_{n}', p_buf.at[3, hi, cols], tb.at[hi, cols], left)
-        remote(f'w1_{n}', p_buf.at[2, lo, cols], far.at[lo, cols], right)
-        remote(f'w2_{n}', p_buf.at[2, hi, cols], far.at[hi, cols], left)
+    for n, part in enumerate('ab'):
+        for k, q, device in ((1, n, right), (2, n + 2, left)):
+            rows = pl.ds(q * quarter, quarter)
+            back = (q + 2) % 4
+            remote(f'i{k}{part}', p_buf.at[1, place(1, 0, back)], near.at[pl.ds(back * quarter, quarter)], device)
+            remote(f'o{k}{part}', p_buf.at[3, place(3, 0, q)], tb.at[rows], device)
+            remote(f'w{k}{part}', p_buf.at[2, rows], far.at[rows], device)
 
     load('hid', hidden, v_hid)
     load('mn', moe_norm, v_mn)
@@ -142,7 +149,7 @@
     ready('hid', 'mn')
     x_buf[0, :tokens] = rms_rows(v_hid[...], norm_row(v_mn))
     pl.semaphore_wait(barrier, 3)
-    send('a1a', 'a2a', 'a1b', 'a2b', 'd0')
+    send('a1a', 'a2a', 'd0')
 
     ready('wr', 'ids')
     logits = lax.dot_general(v_wr[...], x_buf[0, :tokens], (((1,), (1,)), ((), ())), preferred_element_type=F32)
@@ -154,7 +161,7 @@
     top = jnp.max(jnp.where(mask, logits, -jnp.inf), axis=0, keepdims=True)
     powers = jnp.where(mask, jnp.exp(logits - top), 0.0)
     g_buf[0, 0] = powers / jnp.sum(powers, axis=0, keepdims=True)
-    send('g1', 'g2', 'gd0', 'a3a', 'a4a')
+    send('g1', 'g2', 'gd0', 'a1b', 'a2b', 'a3a', 'a4a')
 
     ready('an', 'wq', 'wk', 'wv', 'cos', 'sin')
     normed = rms_rows(v_hid[...], norm_row(v_an))
@@ -204,69 +211,83 @@
         gates_c = gt.T
         for e in range(n_local):
             gate = jnp.sum(jnp.where(e_lane == e, gates_c, 0.0), axis=-1, keepdims=True)
-            gate_b[int(c == 0), e, par * tokens:(par + 1) * tokens] = jnp.broadcast_to(gate, (tokens, LANES))
+            gate = jnp.broadcast_to(gate, (tokens, LANES))
+            for q in range(4):
+                gate_b[e, place(c, par, q)] = gate[q * quarter:(q + 1) * quarter]
 
     def act(c, rows, e):
         x = x_buf[c, rows]
-        used = jnp.concatenate([gate_b[int(c == 0), e, rows]] * (COL // LANES), axis=1) > 0.0
+        used = jnp.concatenate([gate_b[e, rows]] * (COL // LANES), axis=1) > 0.0
         for n in range(exp_ff // COL):
             cols = slice(n * COL, (n + 1) * COL)
             z = silu(dot(x, v_eg[e, :, cols])) * dot(x, v_eu[e, :, cols])
-            hb[int(c == 0), rows, e * exp_ff + n * COL:e * exp_ff + (n + 1) * COL] = jnp.where(used, z, 0.0).astype(BF16)
-
-    def down(c, part):
-        for n in range(part * model // N_P // COL, (part + 1) * model // N_P // COL):
+            hb[rows, e * exp_ff + n * COL:e * exp_ff + (n + 1) * COL] = jnp.where(used, z, 0.0).astype(BF16)
+
+    def down(c, rows, col_lo, col_hi):
+        for n in range(col_lo // COL, col_hi // COL):
             cols = slice(n * COL, (n + 1) * COL)
             for e in range(n_local):
-                y = dot(hb[int(c == 0), :, e * exp_ff:(e + 1) * exp_ff], v_ed[e, :, cols]).astype(BF16).astype(F32)
-                y = y * jnp.concatenate([gate_b[int(c == 0), e]] * (COL // LANES), axis=1)
-                p_buf[c, :, cols] = y if e == 0 else p_buf[c, :, cols] + y
-        send(f'p{c}_{part}')
-
-    def add_partner(c, n):
-        recv(f'p{c}_{n}')
-        cols = slice(n * model // N_P, (n + 1) * model // N_P)
-        p_buf[c, :tokens, cols] = p_buf[c, :tokens, cols] + pr_buf[c, :, cols]
+                y = dot(hb[rows, e * exp_ff:(e + 1) * exp_ff], v_ed[e, :, cols]).astype(BF16).astype(F32)
+                y = y * jnp.concatenate([gate_b[e, rows]] * (COL // LANES), axis=1)
+                p_buf[c, rows, cols] = y if e == 0 else p_buf[c, rows, cols] + y
+
+    def down_cols(c):
+        for n in range(N_P):
+            down(c, both, n * model // N_P, (n + 1) * model // N_P)
+            send(f'p{c}_{n}')
+
+    def down_rows(c, n):
+        down(c, slice(n * tokens, (n + 1) * tokens), 0, model)
+        send(f'p{c}' + 'ab'[n])
+
+    def add_cols(c):
+        for n in range(N_P):
+            recv(f'p{c}_{n}')
+        p_buf[c, :tokens] = p_buf[c, :tokens] + pr_buf[c]
+
+    def add_rows(c, n):
+        recv(f'p{c}' + 'ab'[n])
+        rows = slice(n * tokens, n * tokens + half)
+        p_buf[c, rows] = p_buf[c, rows] + pr_buf[c, n * half:(n + 1) * half]
 
     def send_near(n):
-        add_partner(1, n)
-        send(f'i1_{n}', f'i2_{n}')
+        add_rows(1, n)
+        send('i1' + 'ab'[n], 'i2' + 'ab'[n])
 
     def send_far(n):
-        add_partner(3, n)
-        send(*(f'o{k}_{m}' for m in range(n * N_O // N_P, (n + 1) * N_O // N_P) for k in (1, 2)))
+        add_rows(3, n)
+        send('o1' + 'ab'[n], 'o2' + 'ab'[n])
 
     def pass_on(n):
-        cols = slice(n * model // N_O, (n + 1) * model // N_O)
-        recv(f'o1_{n}', f'o2_{n}')
-        p_buf[2, :tokens, cols] = p_buf[2, :tokens, cols] + tb[:, cols]
-        send(f'w1_{n}', f'w2_{n}')
+        recv('o1' + 'ab'[n], 'o2' + 'ab'[n])
+        for q in (n, n + 2):
+            rows = slice(q * quarter, (q + 1) * quarter)
+            p_buf[2, rows] = p_buf[2, rows] + tb[rows]
+        send('w1' + 'ab'[n], 'w2' + 'ab'[n])
 
     def ffn_block(b, x):
         act_cols = slice(b * FF_BLOCK, (b + 1) * FF_BLOCK)
         for n in range(FF_BLOCK // COL):
             cols = slice(b * FF_BLOCK + n * COL, b * FF_BLOCK + (n + 1) * COL)
             z = silu(dot(x, v_fg[:, cols])) * dot(x, v_fu[:, cols])
-            hb[0, :tokens, n * COL:(n + 1) * COL] = z.astype(BF16)
-        h = hb[0, :tokens, :FF_BLOCK]
+            hb[:tokens, n * COL:(n + 1) * COL] = z.astype(BF16)
+        h = hb[:tokens, :FF_BLOCK]
         for n in range(model // COL):
             cols = slice(n * COL, (n + 1) * COL)
             y = dot(h, v_fd[act_cols, cols])
             ffn_acc[:, cols] = y + (att[:, cols].astype(F32) if b == 0 else ffn_acc[:, cols])
 
-    same, other, both = slice(0, tokens), slice(tokens, 2 * tokens), slice(0, 2 * tokens)
+    first, second, both = slice(0, tokens), slice(tokens, 2 * tokens), slice(0, 2 * tokens)
     attend(0)
     attend(1)
     attend(2)
     recv('a1a', 'a2a')
-    send('f1a', 'f2a')
+    send('f1a', 'f2a', 'd1a')
+    recv('g1', 'g2')
+    send('g3', 'gd1', 'gd2')
     attend(3)
     ready('wo', 'fn')
     att[...] = (v_hid[...].astype(F32) + dot(ctx[...], v_wo[...])).astype(BF16)
-    recv('a1b', 'a2b')
-    send('f1b', 'f2b', 'd1')
-    recv('g1', 'g2')
-    send('g3', 'gd1', 'gd2', 'a3b', 'a4b')
 
     n_blk = ff_dim // 1024
     for b in range(n_blk):
@@ -276,69 +297,69 @@
         load(f'fd{b}', ffn_down.at[cols], v_fd.at[cols])
 
     for e in range(n_local):
-        ready(f'eg{e}', f'eu{e}')
+        ready(f'eg{e}', f'eu{e}', f'ed{e}')
+    recv('gd1', 'gd2', 'd1a')
     set_gates(1, 0)
+    set_gates(1, 1)
+    act(1, first, 0)
+    recv('a1b', 'a2b')
+    send('f1b', 'f2b', 'd1b', 'a3b', 'a4b')
+    for e in range(1, n_local):
+        act(1, first, e)
+    down_rows(1, 0)
+    recv('d1b')
+    for e in range(n_local - 1):
+        act(1, second, e)
+    recv('f1a', 'f2a', 'g3')
+    send('d3a', 'gd3')
+    act(1, second, n_local - 1)
+    send_near(0)
+    down_rows(1, 1)
+    recv('gd3', 'd3a')
+    set_gates(3, 0)
+    set_gates(3, 1)
+    act(3, first, 0)
+    act(3, first, 1)
+    recv('f1b', 'f2b')
+    send('d3b')
+    act(3, first, 2)
+    act(3, first, 3)
+    send_near(1)
+    down_rows(3, 0)
+    recv('d3b', 'a3a', 'a3b', 'a4a', 'a4b')
+    send('d2')
     for e in range(n_local):
-        act(1, same, e)
-    recv('gd1', 'gd2', 'd1')
-    for e in range(n_local):
-        ready(f'ed{e}')
-    set_gates(1, 1)
-    for e in range(n_local):
-        act(1, other, e)
-    down(1, 0)
-    down(1, 1)
-    recv('f1a', 'f2a', 'f1b', 'f2b')
-    send('d3')
-    recv('g3')
-    send('gd3')
+        act(3, second, e)
+    send_far(0)
+    down_rows(3, 1)
+    recv('d2')
+    set_gates(2, 0)
+    set_gates(2, 1)
+    act(2, both, 0)
+    act(2, both, 1)
+    send_far(1)
+    act(2, both, 2)
+    act(2, both, 3)
+    down_cols(2)
     recv('d0', 'gd0')
     set_gates(0, 0)
     set_gates(0, 1)
     act(0, both, 0)
-    send_near(0)
     act(0, both, 1)
-    send_near(1)
-    recv('gd3', 'd3')
-    set_gates(3, 0)
-    set_gates(3, 1)
-    for e in range(n_local):
-        act(3, both, e)
-    recv('a3a', 'a3b', 'a4a', 'a4b')
-    send('d2')
-    down(3, 0)
-    down(3, 1)
+    add_cols(2)
+    pass_on(0)
     act(0, both, 2)
-    send_far(0)
     act(0, both, 3)
-    send_far(1)
-    recv('d2')
-    set_gates(2, 0)
-    set_gates(2, 1)
-    for e in range(n_local):
-        act(2, both, e)
-    down(2, 0)
-    down(2, 1)
-    down(0, 0)
-    add_partner(2, 0)
-    pass_on(0)
-    down(0, 1)
-    add_partner(2, 1)
-    pass_on(1)
+    down_cols(0)
     for b in range(n_blk):
         ready(f'fg{b}', f'fu{b}', f'fd{b}')
+    pass_on(1)
     normed_ffn = rms_rows(att[...], norm_row(v_fn))
-    n_ffn = ff_dim // FF_BLOCK
-    for b in range(n_ffn):
+    for b in range(ff_dim // FF_BLOCK):
         ffn_block(b, normed_ffn)
-        if b == 0:
-            pass_on(2)
-        if b == 2:
-            pass_on(3)
-    for n in range(N_P):
-        add_partner(0, n)
-        recv(f'i1_{n}', f'i2_{n}')
-    late = tuple(f'w{k}_{n}' for k in (1, 2) for n in range(N_O))
+    add_cols(0)
+    recv('i1a', 'i2a', 'i1b', 'i2b')
+    late = ('w1a', 'w2a', 'w1b', 'w2b')
     for name, copy in copies.items():
         if name not in late:
             copy.wait_send()
@@ -382,8 +403,8 @@
             pltpu.VMEM((tokens, kv_dim), F32),
             pltpu.VMEM((tokens, kv_dim), F32),
             pltpu.VMEM((tokens, n_heads * head_dim), BF16),
-            pltpu.VMEM((2, 2 * tokens, n_local * exp_ff), BF16),
-            pltpu.VMEM((2, n_local, 2 * tokens, LANES), F32),
+            pltpu.VMEM((2 * tokens, n_local * exp_ff), BF16),
+            pltpu.VMEM((n_local, 2 * tokens, LANES), F32),
             pltpu.VMEM((tokens, model), BF16),
             pltpu.VMEM((tokens, model), F32),
             pltpu.SemaphoreType.DMA((48,)),

time: 36.9 us -> 36.2 us (0.981)
  Pallas kernels: 36.1 us -> 35.3 us
    pallas_call x1, Pallas kernels: 36.1 us -> 35.3 us  [per_device(): pl.pallas_call(functools.partial(kernel, group), out_shape=(pltpu.VMEM((t...]
where the time goes in v5:
time: 36.2 us; the launch traced here: 36.1 us
  Pallas kernels  35.3 us (98%)
  other arithmetic  0.77 us (2%)
    pallas_call x1, Pallas kernels, per_device(): pl.pallas_call(functools.partial(kernel, group), out_shape=(pltpu.VMEM((t...  35.3 us
    reshape x1, other arithmetic, per_device(): return (total + far).astype(BF16).reshape(n_seqs, seq_len, model)  0.77 us

profile of v5, /device:TPU:112, one launch (start us, length us, event | category | flops | bytes accessed | tf_op | source)
XLA Modules:
  0.0 36.1 jit_solution(4912790082614162733)
XLA Ops:
  0.0 35.3 %shard_map.172 = (f32[128,1024]{1,0:T(8,128)S(1)}, f32[128,1024]{1,0:T(8,128)S(1)}) custom-call(bf16[128,1024]{1,0:T(8,128)(2,1)} %bitcast.12, s32[8,128]{1,0:T(8,128)} %bitcast.14, bf16[8,128]{1,0:T(8,128)(2,1)} %bitcast.15, bf16[1024,1024]{1,0:T(8,128)(2,1)} %w_query.1, bf16[1024,512]{1,0:T(8,128)(2,1)} %w_key.1, bf16[1024,512]{1,0:T(8,128)(2,1)} %w_value.1, ...), custom_call_target="tpu_custom_call" | custom-call | tf_op jit(solution)/shard_map/pallas_call | solution.py:414
  35.3 0.8 %fusion = bf16[1,128,1024]{2,1,0:T(8,128)(2,1)} fusion(f32[128,1024]{1,0:T(8,128)S(1)} %get-tuple-element.7, f32[128,1024]{1,0:T(8,128)S(1)} %get-tuple-element.8), kind=kLoop, calls=%fused_computation.1 | loop fusion | flops 262144 | bytes 1310720 | tf_op jit(solution)/shard_map/reshape | solution.py:422

commit v6 on v5

--- a/solution.py
+++ b/solution.py
@@ -213,22 +213,22 @@
             gate = jnp.sum(jnp.where(e_lane == e, gates_c, 0.0), axis=-1, keepdims=True)
             gate = jnp.broadcast_to(gate, (tokens, LANES))
             for q in range(4):
-                gate_b[e, place(c, par, q)] = gate[q * quarter:(q + 1) * quarter]
+                gate_b[int(c == 0), e, place(c, par, q)] = gate[q * quarter:(q + 1) * quarter]
 
     def act(c, rows, e):
         x = x_buf[c, rows]
-        used = jnp.concatenate([gate_b[e, rows]] * (COL // LANES), axis=1) > 0.0
+        used = jnp.concatenate([gate_b[int(c == 0), e, rows]] * (COL // LANES), axis=1) > 0.0
         for n in range(exp_ff // COL):
             cols = slice(n * COL, (n + 1) * COL)
             z = silu(dot(x, v_eg[e, :, cols])) * dot(x, v_eu[e, :, cols])
-            hb[rows, e * exp_ff + n * COL:e * exp_ff + (n + 1) * COL] = jnp.where(used, z, 0.0).astype(BF16)
+            hb[int(c == 0), rows, e * exp_ff + n * COL:e * exp_ff + (n + 1) * COL] = jnp.where(used, z, 0.0).astype(BF16)
 
     def down(c, rows, col_lo, col_hi):
         for n in range(col_lo // COL, col_hi // COL):
             cols = slice(n * COL, (n + 1) * COL)
             for e in range(n_local):
-                y = dot(hb[rows, e * exp_ff:(e + 1) * exp_ff], v_ed[e, :, cols]).astype(BF16).astype(F32)
-                y = y * jnp.concatenate([gate_b[e, rows]] * (COL // LANES), axis=1)
+                y = dot(hb[int(c == 0), rows, e * exp_ff:(e + 1) * exp_ff], v_ed[e, :, cols]).astype(BF16).astype(F32)
+                y = y * jnp.concatenate([gate_b[int(c == 0), e, rows]] * (COL // LANES), axis=1)
                 p_buf[c, rows, cols] = y if e == 0 else p_buf[c, rows, cols] + y
 
     def down_cols(c):
@@ -270,8 +270,8 @@
         for n in range(FF_BLOCK // COL):
             cols = slice(b * FF_BLOCK + n * COL, b * FF_BLOCK + (n + 1) * COL)
             z = silu(dot(x, v_fg[:, cols])) * dot(x, v_fu[:, cols])
-            hb[:tokens, n * COL:(n + 1) * COL] = z.astype(BF16)
-        h = hb[:tokens, :FF_BLOCK]
+            hb[0, :tokens, n * COL:(n + 1) * COL] = z.astype(BF16)
+        h = hb[0, :tokens, :FF_BLOCK]
         for n in range(model // COL):
             cols = slice(n * COL, (n + 1) * COL)
             y = dot(h, v_fd[act_cols, cols])
@@ -283,9 +283,9 @@
     attend(2)
     recv('a1a', 'a2a')
     send('f1a', 'f2a', 'd1a')
+    attend(3)
     recv('g1', 'g2')
     send('g3', 'gd1', 'gd2')
-    attend(3)
     ready('wo', 'fn')
     att[...] = (v_hid[...].astype(F32) + dot(ctx[...], v_wo[...])).astype(BF16)
 
@@ -296,8 +296,13 @@
         load(f'fu{b}', ffn_up.at[:, cols], v_fu.at[:, cols])
         load(f'fd{b}', ffn_down.at[cols], v_fd.at[cols])
 
-    for e in range(n_local):
-        ready(f'eg{e}', f'eu{e}', f'ed{e}')
+    ready('eg0', 'eu0')
+    recv('d0', 'gd0')
+    set_gates(0, 0)
+    set_gates(0, 1)
+    act(0, both, 0)
+    for e in range(1, n_local):
+        ready(f'eg{e}', f'eu{e}')
     recv('gd1', 'gd2', 'd1a')
     set_gates(1, 0)
     set_gates(1, 1)
@@ -306,6 +311,8 @@
     send('f1b', 'f2b', 'd1b', 'a3b', 'a4b')
     for e in range(1, n_local):
         act(1, first, e)
+    for e in range(n_local):
+        ready(f'ed{e}')
     down_rows(1, 0)
     recv('d1b')
     for e in range(n_local - 1):
@@ -341,14 +348,10 @@
     act(2, both, 2)
     act(2, both, 3)
     down_cols(2)
-    recv('d0', 'gd0')
-    set_gates(0, 0)
-    set_gates(0, 1)
-    act(0, both, 0)
     act(0, both, 1)
+    act(0, both, 2)
     add_cols(2)
     pass_on(0)
-    act(0, both, 2)
     act(0, both, 3)
     down_cols(0)
     for b in range(n_blk):
@@ -403,8 +406,8 @@
             pltpu.VMEM((tokens, kv_dim), F32),
             pltpu.VMEM((tokens, kv_dim), F32),
             pltpu.VMEM((tokens, n_heads * head_dim), BF16),
-            pltpu.VMEM((2 * tokens, n_local * exp_ff), BF16),
-            pltpu.VMEM((n_local, 2 * tokens, LANES), F32),
+            pltpu.VMEM((2, 2 * tokens, n_local * exp_ff), BF16),
+            pltpu.VMEM((2, n_local, 2 * tokens, LANES), F32),
             pltpu.VMEM((tokens, model), BF16),
             pltpu.VMEM((tokens, model), F32),
             pltpu.SemaphoreType.DMA((48,)),

time: 36.2 us -> 36.7 us (1.014)
  Pallas kernels: 35.3 us -> 35.8 us
    pallas_call x1, Pallas kernels: 35.3 us -> 35.8 us  [per_device(): pl.pallas_call(functools.partial(kernel, group), out_shape=(pltpu.VMEM((t...]
where the time goes in v6:
time: 36.7 us; the launch traced here: 36.6 us
  Pallas kernels  35.8 us (98%)
  other arithmetic  0.77 us (2%)
    pallas_call x1, Pallas kernels, per_device(): pl.pallas_call(functools.partial(kernel, group), out_shape=(pltpu.VMEM((t...  35.8 us
    reshape x1, other arithmetic, per_device(): return (total + far).astype(BF16).reshape(n_seqs, seq_len, model)  0.77 us

profile of v6, /device:TPU:112, one launch (start us, length us, event | category | flops | bytes accessed | tf_op | source)
XLA Modules:
  0.0 36.6 jit_solution(13552135998584698855)
XLA Ops:
  0.0 35.8 %shard_map.172 = (f32[128,1024]{1,0:T(8,128)S(1)}, f32[128,1024]{1,0:T(8,128)S(1)}) custom-call(bf16[128,1024]{1,0:T(8,128)(2,1)} %bitcast.12, s32[8,128]{1,0:T(8,128)} %bitcast.14, bf16[8,128]{1,0:T(8,128)(2,1)} %bitcast.15, bf16[1024,1024]{1,0:T(8,128)(2,1)} %w_query.1, bf16[1024,512]{1,0:T(8,128)(2,1)} %w_key.1, bf16[1024,512]{1,0:T(8,128)(2,1)} %w_value.1, ...), custom_call_target="tpu_custom_call" | custom-call | tf_op jit(solution)/shard_map/pallas_call | solution.py:417
  35.8 0.8 %fusion = bf16[1,128,1024]{2,1,0:T(8,128)(2,1)} fusion(f32[128,1024]{1,0:T(8,128)S(1)} %get-tuple-element.7, f32[128,1024]{1,0:T(8,128)S(1)} %get-tuple-element.8), kind=kLoop, calls=%fused_computation.1 | loop fusion | flops 262144 | bytes 1310720 | tf_op jit(solution)/shard_map/reshape | solution.py:425

commit v7 on v5

--- a/solution.py
+++ b/solution.py
@@ -88,7 +88,7 @@
     al, ot = pl.ds(0, tokens), pl.ds(tokens, tokens)
 
     def place(c, par, q):
-        if c in (0, 2):
+        if c == 0:
             return pl.ds(par * tokens + q * quarter, quarter)
         return pl.ds((q % 2) * tokens + par * half + (q // 2) * quarter, quarter)
 
@@ -98,11 +98,10 @@
             ('f1a', 1, 0, 3, right), ('f1b', 1, 1, 3, right), ('f2a', 1, 2, 3, left), ('f2b', 1, 3, 3, left)):
         remote(name, x_buf.at[c_src, place(c_src, 0, q)], x_buf.at[c_dst, place(c_dst, 0, q)], device)
     p_cols = [pl.ds(n * model // N_P, model // N_P) for n in range(N_P)]
-    for c in (0, 2):
-        remote(f'd{c}', x_buf.at[c, al], x_buf.at[c, ot], partner)
-        for n, cols in enumerate(p_cols):
-            remote(f'p{c}_{n}', p_buf.at[c, ot, cols], pr_buf.at[c, :, cols], partner)
-    for c in (1, 3):
+    remote('d0', x_buf.at[0, al], x_buf.at[0, ot], partner)
+    for n, cols in enumerate(p_cols):
+        remote(f'p0_{n}', p_buf.at[0, ot, cols], pr_buf.at[0, :, cols], partner)
+    for c in (1, 2, 3):
         for n, part in enumerate('ab'):
             remote(f'd{c}{part}', x_buf.at[c, pl.ds(n * tokens, half)], x_buf.at[c, pl.ds(n * tokens + half, half)], partner)
             remote(f'p{c}{part}', p_buf.at[c, pl.ds(n * tokens + half, half)], pr_buf.at[c, pl.ds(n * half, half)], partner)
@@ -117,7 +116,7 @@
             back = (q + 2) % 4
             remote(f'i{k}{part}', p_buf.at[1, place(1, 0, back)], near.at[pl.ds(back * quarter, quarter)], device)
             remote(f'o{k}{part}', p_buf.at[3, place(3, 0, q)], tb.at[rows], device)
-            remote(f'w{k}{part}', p_buf.at[2, rows], far.at[rows], device)
+            remote(f'w{k}{part}', p_buf.at[2, place(2, 0, q)], far.at[rows], device)
 
     load('hid', hidden, v_hid)
     load('mn', moe_norm, v_mn)
@@ -135,12 +134,12 @@
     for peer in (partner, left, right):
         pl.semaphore_signal(barrier, inc=1, device_id={'ep': peer}, device_id_type=MESH)
 
-    load('wo', w_out, v_wo)
     for e in range(n_local):
         load(f'eg{e}', exp_gate.at[e], v_eg.at[e])
         load(f'eu{e}', exp_up.at[e], v_eu.at[e])
     for e in range(n_local):
         load(f'ed{e}', exp_down.at[e], v_ed.at[e])
+    load('wo', w_out, v_wo)
 
     def norm_row(ref):
         scale = ref[...].astype(F32)
@@ -261,8 +260,7 @@
     def pass_on(n):
         recv('o1' + 'ab'[n], 'o2' + 'ab'[n])
         for q in (n, n + 2):
-            rows = slice(q * quarter, (q + 1) * quarter)
-            p_buf[2, rows] = p_buf[2, rows] + tb[rows]
+            p_buf[2, place(2, 0, q)] = p_buf[2, place(2, 0, q)] + tb[q * quarter:(q + 1) * quarter]
         send('w1' + 'ab'[n], 'w2' + 'ab'[n])
 
     def ffn_block(b, x):
@@ -286,8 +284,6 @@
     recv('g1', 'g2')
     send('g3', 'gd1', 'gd2')
     attend(3)
-    ready('wo', 'fn')
-    att[...] = (v_hid[...].astype(F32) + dot(ctx[...], v_wo[...])).astype(BF16)
 
     n_blk = ff_dim // 1024
     for b in range(n_blk):
@@ -297,7 +293,7 @@
         load(f'fd{b}', ffn_down.at[cols], v_fd.at[cols])
 
     for e in range(n_local):
-        ready(f'eg{e}', f'eu{e}', f'ed{e}')
+        ready(f'eg{e}', f'eu{e}')
     recv('gd1', 'gd2', 'd1a')
     set_gates(1, 0)
     set_gates(1, 1)
@@ -306,6 +302,8 @@
     send('f1b', 'f2b', 'd1b', 'a3b', 'a4b')
     for e in range(1, n_local):
         act(1, first, e)
+    for e in range(n_local):
+        ready(f'ed{e}')
     down_rows(1, 0)
     recv('d1b')
     for e in range(n_local - 1):
@@ -326,35 +324,40 @@
     act(3, first, 3)
     send_near(1)
     down_rows(3, 0)
-    recv('d3b', 'a3a', 'a3b', 'a4a', 'a4b')
-    send('d2')
+    recv('d3b', 'a3a', 'a4a', 'a3b', 'a4b')
+    send('d2a', 'd2b')
     for e in range(n_local):
         act(3, second, e)
     send_far(0)
     down_rows(3, 1)
-    recv('d2')
+    recv('d2a')
     set_gates(2, 0)
     set_gates(2, 1)
-    act(2, both, 0)
-    act(2, both, 1)
+    for e in range(n_local):
+        act(2, first, e)
     send_far(1)
-    act(2, both, 2)
-    act(2, both, 3)
-    down_cols(2)
+    down_rows(2, 0)
+    recv('d2b')
+    for e in range(n_local):
+        act(2, second, e)
+    add_rows(2, 0)
+    pass_on(0)
+    down_rows(2, 1)
     recv('d0', 'gd0')
     set_gates(0, 0)
     set_gates(0, 1)
     act(0, both, 0)
     act(0, both, 1)
-    add_cols(2)
-    pass_on(0)
+    add_rows(2, 1)
+    pass_on(1)
     act(0, both, 2)
     act(0, both, 3)
     down_cols(0)
+    ready('wo', 'fn')
+    att[...] = (v_hid[...].astype(F32) + dot(ctx[...], v_wo[...])).astype(BF16)
+    normed_ffn = rms_rows(att[...], norm_row(v_fn))
     for b in range(n_blk):
         ready(f'fg{b}', f'fu{b}', f'fd{b}')
-    pass_on(1)
-    normed_ffn = rms_rows(att[...], norm_row(v_fn))
     for b in range(ff_dim // FF_BLOCK):
         ffn_block(b, normed_ffn)
     add_cols(0)

time: 36.2 us -> 38.3 us (1.058)
  Pallas kernels: 35.3 us -> 37.4 us
    pallas_call x1, Pallas kernels: 35.3 us -> 37.4 us  [per_device(): pl.pallas_call(functools.partial(kernel, group), out_shape=(pltpu.VMEM((t...]
where the time goes in v7:
time: 38.3 us; the launch traced here: 38.2 us
  Pallas kernels  37.4 us (98%)
  other arithmetic  0.77 us (2%)
    pallas_call x1, Pallas kernels, per_device(): pl.pallas_call(functools.partial(kernel, group), out_shape=(pltpu.VMEM((t...  37.4 us

profile of v7, /device:TPU:112, one launch (start us, length us, event | category | flops | bytes accessed | tf_op | source)
XLA Modules:
  0.0 38.2 jit_solution(3720752709274192727)
XLA Ops:
  0.0 37.4 %shard_map.172 = (f32[128,1024]{1,0:T(8,128)S(1)}, f32[128,1024]{1,0:T(8,128)S(1)}) custom-call(bf16[128,1024]{1,0:T(8,128)(2,1)} %bitcast.12, s32[8,128]{1,0:T(8,128)} %bitcast.14, bf16[8,128]{1,0:T(8,128)(2,1)} %bitcast.15, bf16[1024,1024]{1,0:T(8,128)(2,1)} %w_query.1, bf16[1024,512]{1,0:T(8,128)(2,1)} %w_key.1, bf16[1024,512]{1,0:T(8,128)(2,1)} %w_value.1, ...), custom_call_target="tpu_custom_call" | custom-call | tf_op jit(solution)/shard_map/pallas_call | solution.py:417
  37.4 0.8 %fusion = bf16[1,128,1024]{2,1,0:T(8,128)(2,1)} fusion(f32[128,1024]{1,0:T(8,128)S(1)} %get-tuple-element.7, f32[128,1024]{1,0:T(8,128)S(1)} %get-tuple-element.8), kind=kLoop, calls=%fused_computation.1 | loop fusion | flops 262144 | bytes 1310720 | tf_op jit(solution)/shard_map/reshape | solution.py:425

commit v8 on v5

--- a/solution.py
+++ b/solution.py
@@ -13,7 +13,7 @@
 MESH = pl.DeviceIdType.MESH
 F32, BF16 = jnp.float32, jnp.bfloat16
 LANES = 128
-FF_BLOCK = 512
+FF_BLOCK = 1024
 COL = 256
 N_P = 2
 VMEM_BYTES = 60 * 1024 * 1024
@@ -105,7 +105,12 @@
     for c in (1, 3):
         for n, part in enumerate('ab'):
             remote(f'd{c}{part}', x_buf.at[c, pl.ds(n * tokens, half)], x_buf.at[c, pl.ds(n * tokens + half, half)], partner)
-            remote(f'p{c}{part}', p_buf.at[c, pl.ds(n * tokens + half, half)], pr_buf.at[c, pl.ds(n * half, half)], partner)
+            if c == 1:
+                remote(f'p1{part}', p_buf.at[1, pl.ds(n * tokens + half, half)], pr_buf.at[1, pl.ds(n * half, half)], partner)
+            else:
+                for k, cols in enumerate(p_cols):
+                    remote(f'p3{part}_{k}', p_buf.at[3, pl.ds(n * tokens + half, half), cols],
+                           pr_buf.at[3, pl.ds(n * half, half), cols], partner)
     remote('g1', g_buf.at[0, 0], g_buf.at[1, 0], right)
     remote('g2', g_buf.at[0, 0], g_buf.at[2, 0], left)
     remote('g3', g_buf.at[1, 0], g_buf.at[3, 0], right)
@@ -234,7 +239,7 @@
     def down_cols(c):
         for n in range(N_P):
             down(c, both, n * model // N_P, (n + 1) * model // N_P)
-            send(f'p{c}_{n}')
+            send(*((f'p3a_{n}', f'p3b_{n}') if c == 3 else (f'p{c}_{n}',)))
 
     def down_rows(c, n):
         down(c, slice(n * tokens, (n + 1) * tokens), 0, model)
@@ -246,7 +251,7 @@
         p_buf[c, :tokens] = p_buf[c, :tokens] + pr_buf[c]
 
     def add_rows(c, n):
-        recv(f'p{c}' + 'ab'[n])
+        recv(*(('p1' + 'ab'[n],) if c == 1 else tuple('p3' + 'ab'[n] + f'_{k}' for k in range(N_P))))
         rows = slice(n * tokens, n * tokens + half)
         p_buf[c, rows] = p_buf[c, rows] + pr_buf[c, n * half:(n + 1) * half]
 
@@ -297,7 +302,7 @@
         load(f'fd{b}', ffn_down.at[cols], v_fd.at[cols])
 
     for e in range(n_local):
-        ready(f'eg{e}', f'eu{e}', f'ed{e}')
+        ready(f'eg{e}', f'eu{e}')
     recv('gd1', 'gd2', 'd1a')
     set_gates(1, 0)
     set_gates(1, 1)
@@ -306,6 +311,8 @@
     send('f1b', 'f2b', 'd1b', 'a3b', 'a4b')
     for e in range(1, n_local):
         act(1, first, e)
+    for e in range(n_local):
+        ready(f'ed{e}')
     down_rows(1, 0)
     recv('d1b')
     for e in range(n_local - 1):
@@ -314,29 +321,26 @@
     send('d3a', 'gd3')
     act(1, second, n_local - 1)
     send_near(0)
+    recv('f1b', 'f2b')
+    send('d3b')
     down_rows(1, 1)
-    recv('gd3', 'd3a')
+    recv('gd3', 'd3a', 'd3b')
     set_gates(3, 0)
     set_gates(3, 1)
-    act(3, first, 0)
-    act(3, first, 1)
-    recv('f1b', 'f2b')
-    send('d3b')
-    act(3, first, 2)
-    act(3, first, 3)
+    act(3, both, 0)
+    act(3, both, 1)
     send_near(1)
-    down_rows(3, 0)
-    recv('d3b', 'a3a', 'a3b', 'a4a', 'a4b')
+    recv('a3a', 'a3b', 'a4a', 'a4b')
     send('d2')
-    for e in range(n_local):
-        act(3, second, e)
-    send_far(0)
-    down_rows(3, 1)
+    act(3, both, 2)
+    act(3, both, 3)
+    down_cols(3)
     recv('d2')
     set_gates(2, 0)
     set_gates(2, 1)
     act(2, both, 0)
     act(2, both, 1)
+    send_far(0)
     send_far(1)
     act(2, both, 2)
     act(2, both, 3)

time: 36.2 us -> 37.3 us (1.030)
  Pallas kernels: 35.3 us -> 36.5 us
    pallas_call x1, Pallas kernels: 35.3 us -> 36.5 us  [per_device(): pl.pallas_call(functools.partial(kernel, group), out_shape=(pltpu.VMEM((t...]
where the time goes in v8:
time: 37.3 us; the launch traced here: 37.2 us
  Pallas kernels  36.5 us (98%)
  other arithmetic  0.77 us (2%)
    pallas_call x1, Pallas kernels, per_device(): pl.pallas_call(functools.partial(kernel, group), out_shape=(pltpu.VMEM((t...  36.5 us
    reshape x1, other arithmetic, per_device(): return (total + far).astype(BF16).reshape(n_seqs, seq_len, model)  0.77 us

profile of v8, /device:TPU:112, one launch (start us, length us, event | category | flops | bytes accessed | tf_op | source)
XLA Modules:
  0.0 37.2 jit_solution(17132990891535456772)
XLA Ops:
  0.0 36.5 %shard_map.172 = (f32[128,1024]{1,0:T(8,128)S(1)}, f32[128,1024]{1,0:T(8,128)S(1)}) custom-call(bf16[128,1024]{1,0:T(8,128)(2,1)} %bitcast.12, s32[8,128]{1,0:T(8,128)} %bitcast.14, bf16[8,128]{1,0:T(8,128)(2,1)} %bitcast.15, bf16[1024,1024]{1,0:T(8,128)(2,1)} %w_query.1, bf16[1024,512]{1,0:T(8,128)(2,1)} %w_key.1, bf16[1024,512]{1,0:T(8,128)(2,1)} %w_value.1, ...), custom_call_target="tpu_custom_call" | custom-call | tf_op jit(solution)/shard_map/pallas_call | solution.py:418
  36.5 0.8 %fusion = bf16[1,128,1024]{2,1,0:T(8,128)(2,1)} fusion(f32[128,1024]{1,0:T(8,128)S(1)} %get-tuple-element.7, f32[128,1024]{1,0:T(8,128)S(1)} %get-tuple-element.8), kind=kLoop, calls=%fused_computation.1 | loop fusion | flops 262144 | bytes 1310720 | tf_op jit(solution)/shard_map/reshape | solution.py:426

commit v9 on v5

--- a/solution.py
+++ b/solution.py
@@ -297,7 +297,7 @@
         load(f'fd{b}', ffn_down.at[cols], v_fd.at[cols])
 
     for e in range(n_local):
-        ready(f'eg{e}', f'eu{e}', f'ed{e}')
+        ready(f'eg{e}', f'eu{e}')
     recv('gd1', 'gd2', 'd1a')
     set_gates(1, 0)
     set_gates(1, 1)
@@ -306,6 +306,8 @@
     send('f1b', 'f2b', 'd1b', 'a3b', 'a4b')
     for e in range(1, n_local):
         act(1, first, e)
+    for e in range(n_local):
+        ready(f'ed{e}')
     down_rows(1, 0)
     recv('d1b')
     for e in range(n_local - 1):

time: 36.2 us -> 36.3 us (level)
  no operation moved by 1% of the time
where the time goes in v9:
time: 36.3 us; the launch traced here: 36.2 us
  Pallas kernels  35.4 us (98%)
  other arithmetic  0.77 us (2%)
    pallas_call x1, Pallas kernels, per_device(): pl.pallas_call(functools.partial(kernel, group), out_shape=(pltpu.VMEM((t...  35.4 us
    reshape x1, other arithmetic, per_device(): return (total + far).astype(BF16).reshape(n_seqs, seq_len, model)  0.77 us

profile of v9, /device:TPU:112, one launch (start us, length us, event | category | flops | bytes accessed | tf_op | source)
XLA Modules:
  0.0 36.2 jit_solution(5190791011611129753)
XLA Ops:
  0.0 35.4 %shard_map.172 = (f32[128,1024]{1,0:T(8,128)S(1)}, f32[128,1024]{1,0:T(8,128)S(1)}) custom-call(bf16[128,1024]{1,0:T(8,128)(2,1)} %bitcast.12, s32[8,128]{1,0:T(8,128)} %bitcast.14, bf16[8,128]{1,0:T(8,128)(2,1)} %bitcast.15, bf16[1024,1024]{1,0:T(8,128)(2,1)} %w_query.1, bf16[1024,512]{1,0:T(8,128)(2,1)} %w_key.1, bf16[1024,512]{1,0:T(8,128)(2,1)} %w_value.1, ...), custom_call_target="tpu_custom_call" | custom-call | tf_op jit(solution)/shard_map/pallas_call | solution.py:416
  35.4 0.8 %fusion = bf16[1,128,1024]{2,1,0:T(8,128)(2,1)} fusion(f32[128,1024]{1,0:T(8,128)S(1)} %get-tuple-element.7, f32[128,1024]{1,0:T(8,128)S(1)} %get-tuple-element.8), kind=kLoop, calls=%fused_computation.1 | loop fusion | flops 262144 | bytes 1310720 | tf_op jit(solution)/shard_map/reshape | solution.py:424
